TPU v7x, 32 devices: a whole 2x2x4 slice. The times are simulated.
32 devices in a mesh: dp: 2 (over x), ep: 16 (over z, y, core).
Axes of the slice: x: 2, y: 2, z: 4, core: 2. Of those that a mesh axis runs over, the one named last changes fastest.
Arguments:
- hidden: bfloat16 [65536, 4096], P(('dp', 'ep')), parts along dimension 0
- ln_gamma: float32 [4096], replicated
- ln_beta: float32 [4096], replicated
- w_router: bfloat16 [4096, 16], replicated
- w_gate: bfloat16 [16, 4096, 448], P('ep')
- w_up: bfloat16 [16, 4096, 448], P('ep')
- w_down: bfloat16 [16, 448, 4096], P('ep')
- choice: int32 [65536, 2], P(('dp', 'ep')), parts along dimension 0
- mask_first: int32 [65536, 16], P(('dp', 'ep')), parts along dimension 0
- mask_second: int32 [65536, 16], P(('dp', 'ep')), parts along dimension 0
Outputs:
- output: bfloat16 [65536, 4096], P(('dp', 'ep')), parts along dimension 0
There are 2 independent parts. A program takes and returns all parts, laid end to end along the dimension named above; an argument that names none is the same for every part.
All inputs are finite; a program needn't handle non-finite values.
Results may differ from a plain program's by a relative error of at most 0.001.
Values are sent between devices in bfloat16 or wider.
A program may use at most 1 GiB of HBM per device.

v0:
```python
import jax
import jax.numpy as jnp
from jax import lax
from jax.sharding import PartitionSpec as P

LN_EPS = 1e-5


def layer_norm(token_rows, ln_gamma, ln_beta):
    values = token_rows.astype(jnp.float32)
    centred = values - jnp.mean(values, axis=-1, keepdims=True)
    variance = jnp.mean(centred * centred, axis=-1, keepdims=True)
    return (centred * lax.rsqrt(variance + LN_EPS) * ln_gamma + ln_beta).astype(jnp.bfloat16)


def sparse_gates(normed, w_router, choice, mask_first, mask_second):
    scores = jnp.dot(normed, w_router, preferred_element_type=jnp.float32)
    expert_ids = jnp.arange(w_router.shape[1], dtype=jnp.int32)
    mask_pair = jnp.stack([mask_first, mask_second], axis=1) > 0
    soft_probs = jax.nn.softmax(jnp.where(mask_pair, scores[:, None, :], -jnp.inf), axis=-1)
    return jnp.sum(jnp.where(choice[:, :, None] == expert_ids, soft_probs, 0.0), axis=-1)


def copy_slots(choice, experts, capacity):
    expert_ids = jnp.arange(experts, dtype=jnp.int32)
    hit_count = (choice[..., None] == expert_ids).astype(jnp.int32)
    per_token = jnp.sum(hit_count, axis=-2)
    before = jnp.cumsum(per_token, axis=-2) - per_token
    position = jnp.sum(hit_count * before[..., None, :], axis=-1)
    return position, position < capacity


def expert_mlp(expert_in, w_gate, w_up, w_down):
    gate_proj = jnp.einsum("secd,edf->secf", expert_in, w_gate, preferred_element_type=jnp.float32)
    up_proj = jnp.einsum("secd,edf->secf", expert_in, w_up, preferred_element_type=jnp.float32)
    inner_act = (jax.nn.silu(gate_proj) * up_proj).astype(jnp.bfloat16)
    return jnp.einsum("secf,efd->secd", inner_act, w_down, preferred_element_type=jnp.float32).astype(jnp.bfloat16)


def solution(mesh):
    group_size = mesh.shape["ep"]
    rows_spec = P(("dp", "ep"))

    def device_step(hidden, ln_gamma, ln_beta, w_router, w_gate, w_up, w_down, choice, mask_first, mask_second):
        tokens, row_width = hidden.shape
        local_experts = w_gate.shape[0]
        experts = local_experts * group_size
        capacity = (10 * tokens + 4 * experts - 1) // (4 * experts)
        slot_count = experts * capacity
        normed = layer_norm(hidden, ln_gamma, ln_beta)
        gate_vals = sparse_gates(normed, w_router, choice, mask_first, mask_second)
        position, kept_copy = copy_slots(choice, experts, capacity)
        flat_slot = jnp.where(kept_copy, choice * capacity + position, slot_count)
        token_ids = jnp.broadcast_to(jnp.arange(tokens, dtype=jnp.int32)[:, None], (tokens, 2))
        source_row = jnp.full((slot_count,), tokens, jnp.int32).at[flat_slot.reshape(-1)].set(token_ids.reshape(-1), mode="drop")
        send_rows = jnp.take(normed, source_row, axis=0, mode="fill", fill_value=0)
        recv_rows = lax.all_to_all(send_rows, "ep", 0, 0, tiled=True)
        expert_out = expert_mlp(recv_rows.reshape(group_size, local_experts, capacity, row_width), w_gate, w_up, w_down)
        back_rows = lax.all_to_all(expert_out.reshape(slot_count, row_width), "ep", 0, 0, tiled=True)
        picked = jnp.take(back_rows, flat_slot, axis=0, mode="fill", fill_value=0)
        mixed_out = hidden.astype(jnp.float32) + jnp.sum(gate_vals[:, :, None] * picked.astype(jnp.float32), axis=1)
        return mixed_out.astype(jnp.bfloat16)

    return jax.shard_map(device_step, mesh=mesh,
                         in_specs=(rows_spec, P(), P(), P(), P("ep"), P("ep"), P("ep"), rows_spec, rows_spec, rows_spec),
                         out_specs=rows_spec, check_vma=False)
```

profile of v0, /device:TPU:12, one launch (start us, length us, event | category | flops | bytes accessed | tf_op | source)
XLA Modules:
  0.0 2418.9 jit_solution(4006264515233830117)
XLA Ops:
  0.0 0.8 convert_reduce_fusion.1
  0.8 4.5 reduce-window.6
  6.2 0.8 select_reduce_fusion.1
  7.0 1.3 compare_and_fusion
  8.7 0.6 reshape.110
  9.4 0.5 reshape.136
  9.9 15.5 scatter_custom_fusion
  25.5 6.9 convert_reduce_fusion
  32.3 7.9 fusion.4
  40.3 17.5 fusion.7
  57.8 77.3 %gather_fusion = bf16[5120,4096]{1,0:T(8,128)(2,1)} fusion(bf16[2048,4096]{1,0:T(8,128)(2,1)} %fusion.7, s32[5120]{0:T(1024)S(1)} %fusion.30), kind=kCustom, calls=%fused_computation | custom fusion | bytes 83906560 | tf_op jit(solution)/shard_map/jit(_take)/gather | solution.py:56
  135.1 28.2 %broadcast_select_fusion.1 = bf16[16,320,4096]{2,1,0:T(8,128)(2,1)} fusion(bf16[16,320,4096]{2,1,0:T(8,128)(2,1)} %bitcast.83, pred[16,320]{1,0:T(8,128)(4,1)S(1)} %broadcast_in_dim.76), kind=kLoop, calls=%fused_computation.10 | loop fusion | flops 20971520 | bytes 83891200 | tf_op jit(solution)/shard_map/jit(_take)/select_n | solution.py:56
  163.3 908.8 %all_to_all.15 = bf16[16,320,4096]{2,1,0:T(8,128)(2,1)} all-to-all(bf16[16,320,4096]{2,1,0:T(8,128)(2,1)} %broadcast_select_fusion.1), channel_id=1, replica_groups=mesh['dp'=2,'ep'=16] {'ep'}, dimensions={0} | all-to-all | bytes 83886080 | tf_op jit(solution)/shard_map/all_to_all | solution.py:57
  1072.1 28.1 %fusion.16 = f32[16,320,448]{2,1,0:T(8,128)} fusion(bf16[16,320,4096]{2,1,0:T(8,128)(2,1)} %all_to_all.15, bf16[1,4096,448]{1,2,0:T(8,128)(2,1)S(1)} %copy-done.7), kind=kOutput, calls=%fused_computation.29 | convolution fusion | flops 18790481920 | bytes 54788096 | tf_op jit(solution)/shard_map/secd,edf->secf/dot_general | solution.py:35
  1100.2 53.7 %convolution_convert_fusion = bf16[16,320,4096]{2,1,0:T(8,128)(2,1)} fusion(f32[16,320,448]{2,1,0:T(8,128)} %fusion.16, bf16[16,320,4096]{2,1,0:T(8,128)(2,1)} %all_to_all.15, bf16[1,448,4096]{2,1,0:T(8,128)(2,1)} %param.16, bf16[1,4096,448]{1,2,0:T(8,128)(2,1)} %param.14), kind=kOutput, calls=%fused_computation.18 | convolution fusion | flops 37615697920 | bytes 100401152 | tf_op jit(solution)/shard_map/secf,efd->secd/dot_general | solution.py:37
  1153.9 9.7 all-to-all-start.1
  1163.6 0.5 copy.16
  1164.4 0.5 reshape.126
  1164.9 10.2 fusion.40
  1175.7 889.8 %all-to-all-done.1 = bf16[16,320,4096]{2,1,0:T(8,128)(2,1)} async-done(((bf16[16,320,4096]{2,1,0:T(8,128)(2,1)}), bf16[16,320,4096]{2,1,0:T(8,128)(2,1)}, u32[]{:S(2)}, u32[]{:S(2)}) %all-to-all-start.1) | async-done | bytes 41943072 | tf_op jit(solution)/shard_map/all_to_all | solution.py:59
  2065.6 151.8 %gather_fusion.1 = bf16[4096,4096]{1,0:T(8,128)(2,1)} fusion(bf16[5120,4096]{1,0:T(8,128)(2,1)} %bitcast.21, s32[4096]{0:T(1024)S(1)} %broadcast_clamp_fusion), kind=kCustom, calls=%fused_computation.1 | custom fusion | bytes 67125248 | tf_op jit(solution)/shard_map/jit(_take)/gather | solution.py:60
  2217.4 52.9 %reshape.125 = bf16[2048,2,4096]{2,1,0:T(2,128)(2,1)} reshape(bf16[4096,4096]{1,0:T(8,128)(2,1)} %gather_fusion.1) | data formatting | bytes 67108864 | tf_op jit(solution)/shard_map/jit(_take)/gather | solution.py:60
  2270.3 126.7 %multiply_reduce_fusion = f32[2048,4096]{1,0:T(8,128)} fusion(bf16[2048,2,4096]{2,1,0:T(2,128)(2,1)} %reshape.125, pred[2048,2]{1,0:T(8,128)(4,1)S(1)} %copy.16, f32[2048,2]{1,0:T(8,128)S(1)} %copy.15), kind=kLoop, calls=%fused_computation.5 | loop fusion | flops 58720256 | bytes 67129344 | tf_op jit(solution)/shard_map/reduce_sum | solution.py:61
  2396.9 22.0 fusion.8
  (38 shorter events, 2.3 us)
Async XLA Ops:
  0.0 1164.9 %copy-start = (bf16[4096,16]{0,1:T(8,128)(2,1)S(1)}, bf16[4096,16]{0,1:T(8,128)(2,1)}, u32[]{:S(2)}) copy-start(bf16[4096,16]{0,1:T(8,128)(2,1)} %param.13) | copy-start | bytes 393220
  0.0 40.3 %copy-start.5 = (f32[4096]{0:T(1024)S(1)}, f32[4096]{0:T(1024)}, u32[]{:S(2)}) copy-start(f32[4096]{0:T(1024)} %param.12) | copy-start | bytes 49156
  0.0 40.3 %copy-start.6 = (f32[4096]{0:T(1024)S(1)}, f32[4096]{0:T(1024)}, u32[]{:S(2)}) copy-start(f32[4096]{0:T(1024)} %param.11) | copy-start | bytes 49156
  8.3 49.5 %copy-start.1 = (s32[2048,2]{0,1:T(2,128)}, s32[2048,2]{0,1:T(2,128)S(1)}, u32[]{:S(2)}) copy-start(s32[2048,2]{0,1:T(2,128)S(1)} %get-tuple-element.6) | copy-start | bytes 49156
  163.3 908.8 %copy-start.7 = (bf16[1,4096,448]{1,2,0:T(8,128)(2,1)S(1)}, bf16[1,4096,448]{1,2,0:T(8,128)(2,1)}, u32[]{:S(2)}) copy-start(bf16[1,4096,448]{1,2,0:T(8,128)(2,1)} %param.15) | copy-start | bytes 11010052
  1153.8 9.7 copy-start.4
  1153.8 10.2 copy-start.2
  1153.9 21.3 copy-start.3
  1153.9 21.3 copy-start.8
  1153.9 21.3 copy-start.9
  1153.9 911.7 %all-to-all-start.1 = ((bf16[16,320,4096]{2,1,0:T(8,128)(2,1)}), bf16[16,320,4096]{2,1,0:T(8,128)(2,1)}, u32[]{:S(2)}, u32[]{:S(2)}) async-start(bf16[16,320,4096]{2,1,0:T(8,128)(2,1)} %convolution_convert_fusion), calls=%async_computation.1 | async-start | bytes 83886080 | tf_op jit(solution)/shard_map/all_to_all | solution.py:59
where the time goes:
time: 2420 us
  blocking collectives  909 us (38%)
  waiting for transfers between devices  890 us (37%)
  local copies, waits for them, and re-layouts  301 us (12%)
  other arithmetic  217 us (9%)
  matrix products  92 us (4%)
    all_to_all x1, blocking collectives, device_step(): recv_rows = lax.all_to_all(send_rows, 'ep', 0, 0, tiled=True)  909 us
    all_to_all x1, waiting for transfers between devices, device_step(): lax.all_to_all(expert_out.reshape(slot_count, row_width), 'ep', 0, 0, til...  890 us
    gather x2, local copies, waits for them, and re-layouts, device_step(): picked = jnp.take(back_rows, flat_slot, axis=0, mode='fill', fill_value=0)  205 us
    reduce_sum x1, other arithmetic, device_step(): jnp.sum(gate_vals[:, :, None] * picked.astype(jnp.float32), axis=1)  127 us
    gather x1, local copies, waits for them, and re-layouts, device_step(): send_rows = jnp.take(normed, source_row, axis=0, mode='fill', fill_value=0)  77.3 us
    dot_general x1, matrix products, expert_mlp(): jnp.einsum('secf,efd->secd', inner_act, w_down, preferred_element_type=jn...  53.7 us
  transfers between devices with their start and end apart: 1, of which 1 were waited for; matrix products, arithmetic and copies ran while one was open for 0% of the time, Pallas kernels for 0%

commit v1 on v0

v1 whole, which is shorter than its diff:
```python
import functools

import jax
import jax.numpy as jnp
from jax import lax
from jax.experimental import pallas as pl
from jax.experimental.pallas import tpu as pltpu
from jax.sharding import PartitionSpec as P

LN_EPS = 1e-5


def layer_norm(token_rows, ln_gamma, ln_beta):
    values = token_rows.astype(jnp.float32)
    centred = values - jnp.mean(values, axis=-1, keepdims=True)
    variance = jnp.mean(centred * centred, axis=-1, keepdims=True)
    return (centred * lax.rsqrt(variance + LN_EPS) * ln_gamma + ln_beta).astype(jnp.bfloat16)


def sparse_gates(normed, w_router, choice, mask_first, mask_second):
    scores = jnp.dot(normed, w_router, preferred_element_type=jnp.float32)
    expert_ids = jnp.arange(w_router.shape[1], dtype=jnp.int32)
    gates = []
    for j, mask in enumerate((mask_first, mask_second)):
        probs = jax.nn.softmax(jnp.where(mask > 0, scores, -jnp.inf), axis=-1)
        gates.append(jnp.sum(jnp.where(choice[:, j:j + 1] == expert_ids, probs, 0.0), axis=-1))
    return gates


def copy_slots(choice, experts):
    expert_ids = jnp.arange(experts, dtype=jnp.int32)
    hit_count = (choice[..., None] == expert_ids).astype(jnp.int32)
    per_token = jnp.sum(hit_count, axis=-2)
    before = jnp.cumsum(per_token, axis=-2) - per_token
    return jnp.sum(hit_count * before[..., None, :], axis=-1)


def mix_kernel(width, weight_col, has_prev, n_weights, where, pick_a, pick_b, gate_a, gate_b, act, hidden, *refs):
    weights, refs = refs[:n_weights], refs[n_weights + (1 if has_prev else 0):]
    out, table, mix, x_buf, o_buf, w_buf, w_sem, x_sem, o_sem = refs
    _, capacity, _ = act.shape
    tokens = x_buf.shape[0]
    tiles = width // 128
    step = min(256, width)
    block = mix.shape[0]
    col = pl.multiple_of(where[0], 128)
    load_x = pltpu.make_async_copy(hidden.at[:, pl.ds(col, width)], x_buf, x_sem)
    load_x.start()

    def load_w(source, i, slot):
        return pltpu.make_async_copy(source.at[i, :, pl.ds(weight_col, width)], w_buf.at[slot], w_sem.at[slot])

    for k, source in enumerate(weights):
        count = source.shape[0]
        load_w(source, 0, 0).start()

        @pl.loop(0, count)
        def _(i):
            slot = lax.rem(i, 2)

            @pl.when(i + 1 < count)
            def _():
                load_w(source, i + 1, 1 - slot).start()

            load_w(source, i, slot).wait()
            if n_weights == 1:
                expert = i
            else:
                expert = 2 * i + (where[1] if k == 0 else 1 - where[1])
            rows = pl.ds(pl.multiple_of(expert * capacity, 8), capacity)
            lhs = act[expert]
            for start in range(0, width, step):
                prod = jnp.dot(lhs, w_buf[slot, :, start:start + step], preferred_element_type=jnp.float32)
                prod = prod.astype(jnp.bfloat16).astype(jnp.float32)
                for j in range(step // 128):
                    table[rows, start // 128 + j, :] = prod[:, j * 128:(j + 1) * 128]

    load_x.wait()

    @pl.loop(0, tokens // block)
    def _(b):
        base = pl.multiple_of(b * block, block)

        @pl.loop(0, block // 8)
        def _(i):
            for k in range(8):
                t = base + i * 8 + k
                mix[i * 8 + k] = gate_a[t] * table[pick_a[t]] + gate_b[t] * table[pick_b[t]]

        for j in range(tiles):
            cols = slice(j * 128, (j + 1) * 128)
            total = x_buf[pl.ds(base, block), cols].astype(jnp.float32) + mix[:, j, :]
            o_buf[pl.ds(base, block), cols] = total.astype(jnp.bfloat16)

    store = pltpu.make_async_copy(o_buf, out.at[:, pl.ds(col, width)], o_sem)
    store.start()
    store.wait()


def mix_columns(where, picks, gates, act, hidden, weights, prev, width, weight_col=0):
    experts, capacity, ff_width = act.shape
    tokens = hidden.shape[0]
    tiles = width // 128
    has_prev = prev is not None
    smem, vmem, hbm = [pl.BlockSpec(memory_space=space) for space in (pltpu.SMEM, pltpu.VMEM, pl.ANY)]
    operands = [where, *picks, *gates, act, hidden, *weights] + ([prev] if has_prev else [])
    return pl.pallas_call(
        functools.partial(mix_kernel, width, weight_col, has_prev, len(weights)),
        out_shape=jax.ShapeDtypeStruct(hidden.shape, hidden.dtype),
        in_specs=[smem] * 5 + [vmem] + [hbm] * (len(operands) - 6),
        out_specs=hbm,
        scratch_shapes=[
            pltpu.VMEM((experts * capacity, tiles, 128), jnp.float32),
            pltpu.VMEM((128, tiles, 128), jnp.float32),
            pltpu.VMEM((tokens, width), jnp.bfloat16),
            pltpu.VMEM((tokens, width), jnp.bfloat16),
            pltpu.VMEM((2, ff_width, width), jnp.bfloat16),
            pltpu.SemaphoreType.DMA((2,)),
            pltpu.SemaphoreType.DMA,
            pltpu.SemaphoreType.DMA,
        ],
        input_output_aliases={len(operands) - 1: 0} if has_prev else {},
        cost_estimate=pl.CostEstimate(flops=2 * experts * capacity * ff_width * width,
                                      bytes_accessed=2 * (experts * ff_width * (width + capacity) + 2 * tokens * width),
                                      transcendentals=0),
        compiler_params=pltpu.CompilerParams(vmem_limit_bytes=56 * 1024 * 1024),
    )(*operands)


def solution(mesh):
    group_size = mesh.shape["ep"]
    rows_spec = P(("dp", "ep"))
    partner_pairs = [(k, k ^ 1) for k in range(group_size)]

    def device_step(hidden, ln_gamma, ln_beta, w_router, w_gate, w_up, w_down, choice, mask_first, mask_second):
        tokens, row_width = hidden.shape
        experts = group_size
        chips = group_size // 2
        capacity = (10 * tokens + 4 * experts - 1) // (4 * experts)
        slot_count = experts * capacity
        side = lax.axis_index("dp")
        core = lax.rem(lax.axis_index("ep"), 2)
        on_left, first_core = side == 0, core == 0

        ff_half, col_half = 112, 1280
        ff_split, col_split = 2 * ff_half, 2 * col_half
        wide = 1024

        gate_rows, up_rows, down_rows = w_gate[0].T, w_up[0].T, w_down[0]

        def gather(piece):
            return lax.all_gather(piece[None], "ep", axis=0, tiled=True)

        def swap(mine):
            far = lax.ppermute(mine, "dp", [(0, 1), (1, 0)])
            return far, lax.ppermute(far, "ep", partner_pairs)

        def same_core(own):
            return lax.dynamic_index_in_dim(own.reshape(chips, 2, *own.shape[1:]), core, 1, keepdims=False)

        half_rows = [lax.dynamic_slice_in_dim(w, side * ff_half, ff_half, 0) for w in (gate_rows, up_rows)]
        gu_own = gather(jnp.concatenate(half_rows, axis=0))
        down_own = gather(lax.dynamic_slice_in_dim(down_rows, side * col_half, col_half, 1))
        gate_rest = gather(gate_rows[ff_split:])
        up_rest = gather(up_rows[ff_split:])
        cut_rest = down_rows[:, col_split:]
        down_rest = gather(cut_rest)

        gu_mine = same_core(gu_own)
        gu_far, gu_other = swap(gu_mine)
        even, odd = jnp.where(first_core, gu_far, gu_other), jnp.where(first_core, gu_other, gu_far)
        gu_far = jnp.concatenate([even, odd], axis=1).reshape(gu_own.shape)
        down_mine = same_core(down_own)
        down_wide, down_slim = down_mine[:, :, :wide], down_mine[:, :, wide:]
        down_wide = swap(down_wide)
        down_slim = swap(down_slim)

        normed = layer_norm(hidden, ln_gamma, ln_beta)
        position = copy_slots(choice, experts)
        flat_slot = jnp.where(position < capacity, choice * capacity + position, slot_count)
        token_ids = jnp.broadcast_to(jnp.arange(tokens, dtype=jnp.int32)[:, None], (tokens, 2))
        source_row = jnp.zeros((slot_count,), jnp.int32).at[flat_slot.reshape(-1)].set(token_ids.reshape(-1), mode="drop")
        rows = jnp.take(normed, source_row, axis=0, mode="clip").reshape(experts, capacity, row_width)

        gates = sparse_gates(normed, w_router, choice, mask_first, mask_second)
        gates = [jnp.where(position[:, j] < capacity, gates[j], 0.0) for j in range(2)]
        pick_slot = choice * capacity + jnp.minimum(position, capacity - 1)
        picks = [pick_slot[:, j] for j in range(2)]
        rows, gates, picks = lax.optimization_barrier((rows, gates, picks))

        def project(weight):
            return jnp.einsum("erd,efd->erf", rows, weight, preferred_element_type=jnp.float32)

        def activate(gate_proj, up_proj):
            return (jax.nn.silu(gate_proj) * up_proj).astype(jnp.bfloat16)

        both = project(gu_own)
        act_own = activate(both[:, :, :ff_half], both[:, :, ff_half:])
        both = project(gu_far)
        act_far = activate(both[:, :, :ff_half], both[:, :, ff_half:])
        act_rest = activate(project(gate_rest), project(up_rest))
        act = jnp.concatenate([jnp.where(on_left, act_own, act_far), jnp.where(on_left, act_far, act_own), act_rest], axis=2)

        def place(prev, weights, start, width, weight_col=0):
            where = jnp.stack([jnp.asarray(start, jnp.int32), core.astype(jnp.int32)])
            return mix_columns(where, picks, gates, act, hidden, weights, prev, width, weight_col)

        own_start, far_start = side * col_half, (1 - side) * col_half
        slim, rest = col_half - wide, row_width - col_split - wide
        out = place(None, (down_own,), own_start, wide)
        out = place(out, (down_own,), own_start + wide, slim, wide)
        out = place(out, down_wide, far_start, wide)
        out = place(out, (down_rest,), col_split, wide)
        out = place(out, (down_rest,), col_split + wide, rest, wide)
        return place(out, down_slim, far_start + wide, slim)

    return jax.shard_map(device_step, mesh=mesh,
                         in_specs=(rows_spec, P(), P(), P(), P("ep"), P("ep"), P("ep"), rows_spec, rows_spec, rows_spec),
                         out_specs=rows_spec, check_vma=False)
```

time: 2420 us -> 1040 us (0.43)
  blocking collectives: 909 us -> 0 us
  waiting for transfers between devices: 890 us -> 487 us
  Pallas kernels: 0 us -> 181 us
  local copies, waits for them, and re-layouts: 301 us -> 142 us
  other arithmetic: 217 us -> 89.6 us
  matrix products: 92 us -> 118 us
    all_to_all x1 -> x0, blocking collectives: 909 us -> none  [device_step(): recv_rows = lax.all_to_all(send_rows, 'ep', 0, 0, tiled=True)]
    all_to_all x1 -> x0, waiting for transfers between devices: 890 us -> none  [device_step(): lax.all_to_all(expert_out.reshape(slot_count, row_width), 'ep', 0, 0, til...]
    ppermute x0 -> x6, waiting for transfers between devices: none -> 296 us  [the longest x3 296 us: swap(): far = lax.ppermute(mine, 'dp', [(0, 1), (1, 0)])]
    gather x3 -> x1, local copies, waits for them, and re-layouts: 282 us -> 78.2 us  [device_step(): jnp.take(normed, source_row, axis=0, mode='clip')]
    all_gather x0 -> x5, waiting for transfers between devices: none -> 191 us  [gather(): return lax.all_gather(piece[None], 'ep', axis=0, tiled=True)]
    pallas_call x0 -> x6, Pallas kernels: none -> 181 us  [mix_columns(): pl.pallas_call(functools.partial(mix_kernel, width, weight_col, has_prev,...]
    reduce_sum x2 -> x4, other arithmetic: 127 us -> 0.32 us  [the longest x2 0.17 us: sparse_gates(): jnp.sum(jnp.where(choice[:, j:j + 1] == expert_ids, probs, 0.0), axis=-1)]
    concatenate x0 -> x3, other arithmetic: none -> 26.4 us  [the longest x1 20.1 us: device_step(): gu_far = jnp.concatenate([even, odd], axis=1).reshape(gu_own.shape)]
  transfers between devices with their start and end apart: 1 -> 11, of which waited for: 1 -> 4; matrix products, arithmetic and copies ran while one was open for 0% -> 33% of each run, Pallas kernels for 0% -> 15%
where the time goes in v1:
time: 1040 us
  waiting for transfers between devices  487 us (47%)
  Pallas kernels  181 us (17%)
  local copies, waits for them, and re-layouts  142 us (14%)
  matrix products  118 us (11%)
  other arithmetic  89.6 us (9%)
  between operations  13.7 us (1%)
    ppermute x3, waiting for transfers between devices, swap(): far = lax.ppermute(mine, 'dp', [(0, 1), (1, 0)])  296 us
    all_gather x5, waiting for transfers between devices, gather(): return lax.all_gather(piece[None], 'ep', axis=0, tiled=True)  191 us
    pallas_call x6, Pallas kernels, mix_columns(): pl.pallas_call(functools.partial(mix_kernel, width, weight_col, has_prev,...  181 us
    dot_general x4, matrix products, project(): jnp.einsum('erd,efd->erf', rows, weight, preferred_element_type=jnp.float32)  107 us
    gather x1, local copies, waits for them, and re-layouts, device_step(): jnp.take(normed, source_row, axis=0, mode='clip')  78.2 us
    select_n x1, other arithmetic, device_step(): jnp.where(first_core, gu_far, gu_other)  21.3 us
    squeeze x2, local copies, waits for them, and re-layouts, same_core(): lax.dynamic_index_in_dim(own.reshape(chips, 2, *own.shape[1:]), core, 1,...  21.1 us
  transfers between devices with their start and end apart: 11, of which 4 were waited for; matrix products, arithmetic and copies ran while one was open for 33% of the time, Pallas kernels for 15%

profile of v1, /device:TPU:12, one launch (start us, length us, event | category | flops | bytes accessed | tf_op | source)
XLA Modules:
  0.0 1036.1 jit_solution(18204510983121442951)
XLA Ops:
  21.9 137.8 %all-gather.12.cloned.1.call-done = bf16[3584,4096]{1,0:T(8,128)(2,1)} async-done(((bf16[224,4096]{1,0:T(8,128)(2,1)}), bf16[3584,4096]{1,0:T(8,128)(2,1)}) %all-gather.12.cloned.1.call-update) | async-done | bytes 29360144 | tf_op jit(solution)/shard_map/all_gather | solution.py:152
  159.7 13.4 %dynamic-slice_bitcast_fusion = bf16[8,224,4096]{2,1,0:T(8,128)(2,1)} fusion(bf16[8,2,224,4096]{3,2,1,0:T(8,128)(2,1)} %bitcast.72, s32[]{:T(128)S(6)} %select_n.82), kind=kLoop, calls=%fused_computation.11 | loop fusion | bytes 29360132 | tf_op jit(solution)/shard_map/jit(dynamic_index_in_dim)/squeeze | solution.py:159
  181.7 15.8 %scatter_custom_fusion = s32[5120]{0:T(1024)S(1)} fusion(s32[4096]{0:T(1024)S(1)} %bitcast.95, s32[4096]{0:T(1024)S(1)} %reshape.110, s32[]{:T(128)} %constant.27.clone.1), kind=kCustom, calls=%fused_computation.49 | custom fusion | bytes 20484 | tf_op jit(solution)/shard_map/scatter | solution.py:182
  204.6 53.3 %all-gather.10.cloned.1.call-done.refs_0_ = bf16[16,448,1280]{2,1,0:T(8,128)(2,1)} async-done(((bf16[1,448,1280]{2,1,0:T(8,128)(2,1)}), bf16[16,448,1280]{2,1,0:T(8,128)(2,1)}) %all-gather.10.cloned.1.call-update) | async-done | bytes 18350096 | tf_op jit(solution)/shard_map/all_gather | solution.py:152
  257.8 7.7 dynamic-slice_bitcast_fusion.1
  265.6 8.4 slice.84
  275.5 8.8 fusion.2
  284.4 10.8 %fusion.5 = bf16[2048,4096]{1,0:T(8,128)(2,1)} fusion(bf16[2048,4096]{1,0:T(8,128)(2,1)S(1)} %bitcast.63, f32[4096]{0:T(1024)S(1)} %copy-done.5, f32[4096]{0:T(1024)S(1)} %copy-done.6, f32[2048]{0:T(1024)S(1)} %add_rsqrt_fusion, f32[2048]{0:T(1024)S(1)} %broadcast_multiply_fusion), kind=kLoop, calls=%fused_computation.9 | loop fusion | flops 50331648 | bytes 33603584 | tf_op jit(solution)/shard_map/convert_element_type | solution.py:17
  295.2 78.2 %gather_fusion = bf16[5120,4096]{1,0:T(8,128)(2,1)} fusion(bf16[2048,4096]{1,0:T(8,128)(2,1)} %fusion.5, s32[5120]{0:T(1024)S(1)} %broadcast_clamp_fusion), kind=kCustom, calls=%fused_computation | custom fusion | bytes 83906560 | tf_op jit(solution)/shard_map/jit(_take)/gather | solution.py:183
  373.4 118.2 %collective-permute-done = bf16[8,224,4096]{2,1,0:T(8,128)(2,1)} collective-permute-done((bf16[8,224,4096]{2,1,0:T(8,128)(2,1)}, bf16[8,224,4096]{2,1,0:T(8,128)(2,1)}, u32[]{:S(2)}, u32[]{:S(2)}) %collective-permute-start) | collective-permute-done | bytes 14680096 | tf_op jit(solution)/shard_map/ppermute | solution.py:155
  491.6 10.6 %fusion.14 = (f32[2048]{0:T(1024)S(1)}, f32[2048,16]{0,1:T(8,128)S(1)}) fusion(s32[2048,16]{0,1:T(8,128)S(1)} %copy-done.2, bf16[2048,4096]{1,0:T(8,128)(2,1)} %fusion.5, bf16[4096,16]{0,1:T(8,128)(2,1)S(1)} %copy-done), kind=kOutput, calls=%fused_computation.63 | convolution fusion | flops 268531712 | bytes 17178624 | tf_op jit(solution)/shard_map/dot_general | solution.py:21
  509.4 178.1 %collective-permute-done.2.refs_0_ = bf16[8,448,256]{2,1,0:T(8,128)(2,1)} collective-permute-done((bf16[8,448,256]{2,1,0:T(8,128)(2,1)S(1)}, bf16[8,448,256]{2,1,0:T(8,128)(2,1)}, u32[]{:S(2)}, u32[]{:S(2)}) %collective-permute-start.2) | collective-permute-done | bytes 1835040 | tf_op jit(solution)/shard_map/ppermute | solution.py:155
  688.0 26.9 %fusion.21 = f32[16,320,224]{2,1,0:T(8,128)} fusion(bf16[16,320,4096]{2,1,0:T(8,128)(2,1)} %bitcast.67, bf16[16,224,4096]{2,1,0:T(8,128)(2,1)} %bitcast.96), kind=kOutput, calls=%fused_computation.68 | convolution fusion | flops 9395240960 | bytes 75890688 | tf_op jit(solution)/shard_map/erd,efd->erf/dot_general | solution.py:192
  714.9 26.8 %fusion.19 = f32[16,320,224]{2,1,0:T(8,128)} fusion(bf16[16,320,4096]{2,1,0:T(8,128)(2,1)} %bitcast.68, bf16[16,224,4096]{2,1,0:T(8,128)(2,1)} %bitcast.73), kind=kOutput, calls=%fused_computation.66 | convolution fusion | flops 9395240960 | bytes 75890688 | tf_op jit(solution)/shard_map/erd,efd->erf/dot_general | solution.py:192
  741.7 26.4 %multiply_convert_fusion = bf16[16,320,224]{2,1,0:T(8,128)(2,1)S(1)} fusion(f32[16,320,224]{2,1,0:T(8,128)} %fusion.21, bf16[16,320,4096]{2,1,0:T(8,128)(2,1)} %bitcast.69, bf16[16,224,4096]{2,1,0:T(8,128)(2,1)} %bitcast.97), kind=kOutput, calls=%fused_computation.16 | convolution fusion | flops 9402122240 | bytes 78184448 | tf_op jit(solution)/shard_map/erd,efd->erf/dot_general | solution.py:192
  768.1 21.3 %broadcast_select_fusion.1 = (bf16[8,224,4096]{2,1,0:T(8,128)(2,1)}, bf16[8,224,4096]{2,1,0:T(8,128)(2,1)}) fusion(bf16[8,224,4096]{2,1,0:T(8,128)(2,1)} %collective-permute-done, bf16[8,224,4096]{2,1,0:T(8,128)(2,1)} %collective-permute-done.1, pred[]{:T(512)S(6)} %eq.61), kind=kLoop, calls=%fused_computation.13 | loop fusion | flops 14680064 | bytes 58720256 | tf_op jit(solution)/shard_map/jit(_where)/select_n | solution.py:171
  789.5 20.1 %pad_maximum_fusion = bf16[8,448,4096]{2,1,0:T(8,128)(2,1)} fusion(bf16[8,224,4096]{2,1,0:T(8,128)(2,1)} %get-tuple-element.25, bf16[8,224,4096]{2,1,0:T(8,128)(2,1)} %get-tuple-element.24), kind=kLoop, calls=%fused_computation.10 | loop fusion | flops 58720256 | bytes 58720256 | tf_op jit(solution)/shard_map/concatenate | solution.py:172
  809.6 26.9 %fusion.20 = f32[16,320,224]{2,1,0:T(8,128)} fusion(bf16[16,320,4096]{2,1,0:T(8,128)(2,1)} %bitcast.70, bf16[16,224,4096]{2,1,0:T(8,128)(2,1)} %bitcast.71), kind=kOutput, calls=%fused_computation.67 | convolution fusion | flops 9395240960 | bytes 75890688 | tf_op jit(solution)/shard_map/erd,efd->erf/dot_general | solution.py:192
  848.2 35.8 %shard_map.100.refs_1_ = bf16[2048,4096]{1,0:T(8,128)(2,1)} custom-call(s32[2]{0:T(128)} %pad_add_fusion.5.where, s32[2048]{0:T(1024)} %bitcast.86, s32[2048]{0:T(1024)} %bitcast.80, f32[2048]{0:T(1024)} %get-tuple-element.12.gate_a, f32[2048]{0:T(1024)} %get-tuple-element.13.gate_b, bf16[16,320,448]{2,1,0:T(8,128)(2,1)} %pad_maximum_fusion.1.act, ...), custom_call_target="tpu_custom_call" | custom-call | flops 4697620480 | bytes 27656192 | tf_op jit(solution)/shard_map/pallas_call | solution.py:107
  884.0 22.8 %shard_map.101.refs_2_ = bf16[2048,4096]{1,0:T(8,128)(2,1)} custom-call(s32[2]{0:T(128)} %pad_add_fusion.4.where, s32[2048]{0:T(1024)} %bitcast.87, s32[2048]{0:T(1024)} %bitcast.81, f32[2048]{0:T(1024)} %get-tuple-element.12.gate_a, f32[2048]{0:T(1024)} %get-tuple-element.13.gate_b, ...), custom_call_target="tpu_custom_call", output_to_operand_aliasing={{}: (8, {})} | custom-call | flops 1174405120 | bytes 10354688 | tf_op jit(solution)/shard_map/pallas_call | solution.py:107
  906.8 36.4 %shard_map.102.refs_1_ = bf16[2048,4096]{1,0:T(8,128)(2,1)} custom-call(s32[2]{0:T(128)} %get-tuple-element.37.where, s32[2048]{0:T(1024)} %bitcast.88, s32[2048]{0:T(1024)} %bitcast.82, f32[2048]{0:T(1024)} %get-tuple-element.12.gate_a, f32[2048]{0:T(1024)} %get-tuple-element.13.gate_b, ...), custom_call_target="tpu_custom_call", output_to_operand_aliasing={{}: (9, {})} | custom-call | flops 4697620480 | bytes 27656192 | tf_op jit(solution)/shard_map/pallas_call | solution.py:107
  943.2 35.8 %shard_map.103.refs_1_ = bf16[2048,4096]{1,0:T(8,128)(2,1)} custom-call(s32[2]{0:T(128)} %get-tuple-element.36.where, s32[2048]{0:T(1024)} %bitcast.89, s32[2048]{0:T(1024)} %bitcast.83, f32[2048]{0:T(1024)} %get-tuple-element.12.gate_a, f32[2048]{0:T(1024)} %get-tuple-element.13.gate_b, ...), custom_call_target="tpu_custom_call", output_to_operand_aliasing={{}: (8, {})} | custom-call | flops 4697620480 | bytes 27656192 | tf_op jit(solution)/shard_map/pallas_call | solution.py:107
  979.0 27.4 %shard_map.104.refs_2_ = bf16[2048,4096]{1,0:T(8,128)(2,1)} custom-call(s32[2]{0:T(128)} %get-tuple-element.35.where, s32[2048]{0:T(1024)} %bitcast.90, s32[2048]{0:T(1024)} %bitcast.84, f32[2048]{0:T(1024)} %get-tuple-element.12.gate_a, f32[2048]{0:T(1024)} %get-tuple-element.13.gate_b, ...), custom_call_target="tpu_custom_call", output_to_operand_aliasing={{}: (8, {})} | custom-call | flops 2348810240 | bytes 16121856 | tf_op jit(solution)/shard_map/pallas_call | solution.py:107
  1006.5 22.8 %shard_map.105 = bf16[2048,4096]{1,0:T(8,128)(2,1)} custom-call(s32[2]{0:T(128)} %get-tuple-element.34.where, s32[2048]{0:T(1024)} %bitcast.91, s32[2048]{0:T(1024)} %bitcast.85, f32[2048]{0:T(1024)} %get-tuple-element.12.gate_a, f32[2048]{0:T(1024)} %get-tuple-element.13.gate_b, ...), custom_call_target="tpu_custom_call", output_to_operand_aliasing={{}: (9, {})} | custom-call | flops 1174405120 | bytes 10354688 | tf_op jit(solution)/shard_map/pallas_call | solution.py:107
  (86 shorter events, 52.0 us)
Async XLA Ops:
  6.5 485.1 %copy-start = (bf16[4096,16]{0,1:T(8,128)(2,1)S(1)}, bf16[4096,16]{0,1:T(8,128)(2,1)}, u32[]{:S(2)}) copy-start(bf16[4096,16]{0,1:T(8,128)(2,1)} %param.13) | copy-start | bytes 393220
  6.5 153.1 %all-gather.12.cloned.1.call-start = ((), (), s32[]{:S(2)}) async-start(), calls=%async_computation.1 | async-start | bytes 31195136 | tf_op jit(solution)/shard_map/all_gather | solution.py:152
  10.4 247.4 %all-gather.10.cloned.1.call-start = ((), (), s32[]{:S(2)}) async-start(), calls=%async_computation | async-start | bytes 19496960 | tf_op jit(solution)/shard_map/all_gather | solution.py:152
  12.9 675.1 %all-gather.14.cloned.1.call-start = ((), (), s32[]{:S(2)}) async-start(), calls=%async_computation.2 | async-start | bytes 31195136 | tf_op jit(solution)/shard_map/all_gather | solution.py:152
  15.9 725.8 %all-gather.16.cloned.1.call-start = ((), (), s32[]{:S(2)}) async-start(), calls=%async_computation.3 | async-start | bytes 31195136 | tf_op jit(solution)/shard_map/all_gather | solution.py:152
  18.9 924.3 %all-gather.18.cloned.1.call-start = ((), (), s32[]{:S(2)}) async-start(), calls=%async_computation.4 | async-start | bytes 23396352 | tf_op jit(solution)/shard_map/all_gather | solution.py:152
  159.7 14.9 %copy-start.4 = (s32[2048,2]{0,1:T(2,128)S(1)}, s32[2048,2]{0,1:T(2,128)}, u32[]{:S(2)}) copy-start(s32[2048,2]{0,1:T(2,128)} %param.17) | copy-start | bytes 49156
  173.1 318.5 %collective-permute-start = (bf16[8,224,4096]{2,1,0:T(8,128)(2,1)}, bf16[8,224,4096]{2,1,0:T(8,128)(2,1)}, u32[]{:S(2)}, u32[]{:S(2)}) collective-permute-start(bf16[8,224,4096]{2,1,0:T(8,128)(2,1)} %dynamic-slice_bitcast_fusion), channel_id=1, source_target_pairs={{0,16},{16,0},{1,17},{17,1},{2,18},{18,2},{3,19},{19,3},{4,20},{20... | collective-permute-start | bytes 44040200 | tf_op jit(solution)/shard_map/ppermute | solution.py:155
  265.5 18.7 %slice-start = ((s8[16777216]{0:T(1024)(128)(4,1)}), s8[4194304]{0:T(1024)(128)(4,1)S(1)}, s32[]{:S(2)}) async-start(s8[16777216]{0:T(1024)(128)(4,1)} %bitcast.62), calls=%async_computation.5 | async-start | bytes 8388608
  265.6 18.8 %slice-start.1 = ((s8[16777216]{0:T(1024)(128)(4,1)}), s8[4194304]{0:T(1024)(128)(4,1)S(1)}, s32[]{:S(2)}) async-start(s8[16777216]{0:T(1024)(128)(4,1)} %bitcast.62), calls=%async_computation.6 | async-start | bytes 8388608
  274.0 10.3 slice-start.2
  274.0 10.4 slice-start.3
  274.0 10.4 %copy-start.5 = (f32[4096]{0:T(1024)S(1)}, f32[4096]{0:T(1024)}, u32[]{:S(2)}) copy-start(f32[4096]{0:T(1024)} %param.12) | copy-start | bytes 49156
  274.0 10.4 %copy-start.6 = (f32[4096]{0:T(1024)S(1)}, f32[4096]{0:T(1024)}, u32[]{:S(2)}) copy-start(f32[4096]{0:T(1024)} %param.11) | copy-start | bytes 49156
  274.0 413.5 %collective-permute-start.4 = (bf16[8,448,1024]{2,1,0:T(8,128)(2,1)}, bf16[8,448,1024]{2,1,0:T(8,128)(2,1)}, u32[]{:S(2)}, u32[]{:S(2)}) collective-permute-start(bf16[8,448,1024]{2,1,0:T(8,128)(2,1)} %slice.84), channel_id=1, source_target_pairs={{0,16},{16,0},{1,17},{17,1},{2,18},{18,2},{3,19},{19,3},{4,20},{20... | collective-permute-start | bytes 22020104 | tf_op jit(solution)/shard_map/ppermute | solution.py:155
  295.2 196.4 %copy-start.2 = (s32[2048,16]{0,1:T(8,128)S(1)}, s32[2048,16]{0,1:T(8,128)}, u32[]{:S(2)}) copy-start(s32[2048,16]{0,1:T(8,128)} %param.19) | copy-start | bytes 393220
  373.4 128.8 %copy-start.3 = (s32[2048,16]{0,1:T(8,128)S(1)}, s32[2048,16]{0,1:T(8,128)}, u32[]{:S(2)}) copy-start(s32[2048,16]{0,1:T(8,128)} %param.18) | copy-start | bytes 393220
  491.6 276.5 %collective-permute-start.1 = (bf16[8,224,4096]{2,1,0:T(8,128)(2,1)}, bf16[8,224,4096]{2,1,0:T(8,128)(2,1)}, u32[]{:S(2)}, u32[]{:S(2)}) collective-permute-start(bf16[8,224,4096]{2,1,0:T(8,128)(2,1)} %collective-permute-done), channel_id=1, source_target_pairs={{0,1},{1,0},{2,3},{3,2},{4,5},{5,4},{6,7},{7,6},{8,9},{9,8},{10,11... | collective-permute-start | bytes 44040200 | tf_op jit(solution)/shard_map/ppermute | solution.py:156
  504.0 183.5 %collective-permute-start.2 = (bf16[8,448,256]{2,1,0:T(8,128)(2,1)S(1)}, bf16[8,448,256]{2,1,0:T(8,128)(2,1)}, u32[]{:S(2)}, u32[]{:S(2)}) collective-permute-start(bf16[8,448,256]{2,1,0:T(8,128)(2,1)S(1)} %slice.82), channel_id=1, source_target_pairs={{0,16},{16,0},{1,17},{17,1},{2,18},{18,2},{3,19},{19,3},{4,20},{20... | collective-permute-start | bytes 5505032 | tf_op jit(solution)/shard_map/ppermute | solution.py:155
  687.5 319.0 %collective-permute-start.3 = (bf16[8,448,256]{2,1,0:T(8,128)(2,1)}, bf16[8,448,256]{2,1,0:T(8,128)(2,1)}, u32[]{:S(2)}, u32[]{:S(2)}) collective-permute-start(bf16[8,448,256]{2,1,0:T(8,128)(2,1)} %collective-permute-done.2.refs_0_), channel_id=1, source_target_pairs={{0,1},{1,0},{2,3},{3,2},{4,5},{5,4},{6,7},{7,6},{8,9},{9,8},{10,11... | collective-permute-start | bytes 5505032 | tf_op jit(solution)/shard_map/ppermute | solution.py:156
  687.5 219.3 %collective-permute-start.5 = (bf16[8,448,1024]{2,1,0:T(8,128)(2,1)}, bf16[8,448,1024]{2,1,0:T(8,128)(2,1)}, u32[]{:S(2)}, u32[]{:S(2)}) collective-permute-start(bf16[8,448,1024]{2,1,0:T(8,128)(2,1)} %collective-permute-done.4.refs_0_), channel_id=1, source_target_pairs={{0,1},{1,0},{2,3},{3,2},{4,5},{5,4},{6,7},{7,6},{8,9},{9,8},{10,11... | collective-permute-start | bytes 22020104 | tf_op jit(solution)/shard_map/ppermute | solution.py:156
  1006.5 22.8 %copy-start.1 = (bf16[4096,16]{0,1:T(8,128)(2,1)S(1)}, bf16[4096,16]{0,1:T(8,128)(2,1)}, u32[]{:S(2)}) copy-start(bf16[4096,16]{0,1:T(8,128)(2,1)} %param.13) | copy-start | bytes 393220
Sparse Core Ops, SparseCore 0:
  10.6 149.0 all-gather.11
  161.3 96.5 all-gather.9
  259.4 148.1 all-gather.13
  409.1 148.2 all-gather.15
  558.8 113.7 all-gather.17

commit v2 on v1

--- a/solution.py
+++ b/solution.py
@@ -81,11 +81,13 @@
     def _(b):
         base = pl.multiple_of(b * block, block)
 
-        @pl.loop(0, block // 8)
+        @pl.loop(0, block // 16)
         def _(i):
-            for k in range(8):
-                t = base + i * 8 + k
-                mix[i * 8 + k] = gate_a[t] * table[pick_a[t]] + gate_b[t] * table[pick_b[t]]
+            slots = [base + i * 16 + k for k in range(16)]
+            picked = [(table[pick_a[t]], table[pick_b[t]]) for t in slots]
+            sums = [gate_a[t] * first + gate_b[t] * second for t, (first, second) in zip(slots, picked)]
+            for k in range(16):
+                mix[i * 16 + k] = sums[k]
 
         for j in range(tiles):
             cols = slice(j * 128, (j + 1) * 128)
@@ -168,8 +170,6 @@
 
         gu_mine = same_core(gu_own)
         gu_far, gu_other = swap(gu_mine)
-        even, odd = jnp.where(first_core, gu_far, gu_other), jnp.where(first_core, gu_other, gu_far)
-        gu_far = jnp.concatenate([even, odd], axis=1).reshape(gu_own.shape)
         down_mine = same_core(down_own)
         down_wide, down_slim = down_mine[:, :, :wide], down_mine[:, :, wide:]
         down_wide = swap(down_wide)
@@ -188,16 +188,24 @@
         picks = [pick_slot[:, j] for j in range(2)]
         rows, gates, picks = lax.optimization_barrier((rows, gates, picks))
 
-        def project(weight):
+        by_core = rows.reshape(chips, 2, capacity, row_width)
+        rows_mine = lax.dynamic_index_in_dim(by_core, core, 1, keepdims=False)
+        rows_other = lax.dynamic_index_in_dim(by_core, 1 - core, 1, keepdims=False)
+
+        def project(weight, rows=rows):
             return jnp.einsum("erd,efd->erf", rows, weight, preferred_element_type=jnp.float32)
 
         def activate(gate_proj, up_proj):
             return (jax.nn.silu(gate_proj) * up_proj).astype(jnp.bfloat16)
 
-        both = project(gu_own)
-        act_own = activate(both[:, :, :ff_half], both[:, :, ff_half:])
-        both = project(gu_far)
-        act_far = activate(both[:, :, :ff_half], both[:, :, ff_half:])
+        def activate_both(both):
+            return activate(both[:, :, :ff_half], both[:, :, ff_half:])
+
+        act_own = activate_both(project(gu_own))
+        act_mine = activate_both(project(gu_far, rows_mine))
+        act_other = activate_both(project(gu_other, rows_other))
+        even, odd = jnp.where(first_core, act_mine, act_other), jnp.where(first_core, act_other, act_mine)
+        act_far = jnp.concatenate([even, odd], axis=1).reshape(act_own.shape)
         act_rest = activate(project(gate_rest), project(up_rest))
         act = jnp.concatenate([jnp.where(on_left, act_own, act_far), jnp.where(on_left, act_far, act_own), act_rest], axis=2)
 

time: 1040 us -> 1000 us (0.962)
  other arithmetic: 89.6 us -> 44.3 us
    concatenate x1, other arithmetic: 20.1 us -> 0.26 us  [device_step(): act_far = jnp.concatenate([even, odd], axis=1).reshape(act_own.shape)]
    select_n x1 -> x2, other arithmetic: 21.3 us -> 3.07 us  [the longest x1 3 us: device_step(): jnp.where(first_core, act_mine, act_other)]
    dot_general x4 -> x5, matrix products: 107 us -> 113 us  [project(): jnp.einsum('erd,efd->erf', rows, weight, preferred_element_type=jnp.float32)]
  transfers between devices with their start and end apart: 11 -> 11, of which waited for: 4 -> 4; matrix products, arithmetic and copies ran while one was open for 33% -> 30% of each run, Pallas kernels for 15% -> 16%
where the time goes in v2:
time: 1000 us; the launch traced here: 994 us
  waiting for transfers between devices  494 us (49%)
  Pallas kernels  177 us (18%)
  local copies, waits for them, and re-layouts  143 us (14%)
  matrix products  117 us (12%)
  other arithmetic  44.3 us (4%)
  between operations  13.9 us (1%)
    ppermute x3, waiting for transfers between devices, swap(): far = lax.ppermute(mine, 'dp', [(0, 1), (1, 0)])  303 us
    all_gather x5, waiting for transfers between devices, gather(): return lax.all_gather(piece[None], 'ep', axis=0, tiled=True)  191 us
    pallas_call x6, Pallas kernels, mix_columns(): pl.pallas_call(functools.partial(mix_kernel, width, weight_col, has_prev,...  177 us
    dot_general x5, matrix products, project(): jnp.einsum('erd,efd->erf', rows, weight, preferred_element_type=jnp.float32)  113 us
    gather x1, local copies, waits for them, and re-layouts, device_step(): jnp.take(normed, source_row, axis=0, mode='clip')  77.8 us
    squeeze x2, local copies, waits for them, and re-layouts, same_core(): lax.dynamic_index_in_dim(own.reshape(chips, 2, *own.shape[1:]), core, 1,...  21.2 us
  transfers between devices with their start and end apart: 11, of which 4 were waited for; matrix products, arithmetic and copies ran while one was open for 30% of the time, Pallas kernels for 16%

profile of v2, /device:TPU:12, one launch (start us, length us, event | category | flops | bytes accessed | tf_op | source)
XLA Modules:
  0.0 994.4 jit_solution(12449998610134303475)
XLA Ops:
  21.9 137.8 %all-gather.12.cloned.1.call-done = bf16[3584,4096]{1,0:T(8,128)(2,1)} async-done(((bf16[224,4096]{1,0:T(8,128)(2,1)}), bf16[3584,4096]{1,0:T(8,128)(2,1)}) %all-gather.12.cloned.1.call-update) | async-done | bytes 29360144 | tf_op jit(solution)/shard_map/all_gather | solution.py:154
  159.7 13.4 %dynamic-slice_bitcast_fusion = bf16[8,224,4096]{2,1,0:T(8,128)(2,1)} fusion(bf16[8,2,224,4096]{3,2,1,0:T(8,128)(2,1)} %bitcast.87, s32[]{:T(128)S(6)} %select_n.87), kind=kLoop, calls=%fused_computation.16 | loop fusion | bytes 29360132 | tf_op jit(solution)/shard_map/jit(dynamic_index_in_dim)/squeeze | solution.py:161
  181.6 16.1 %scatter_custom_fusion = s32[5120]{0:T(1024)S(1)} fusion(s32[4096]{0:T(1024)S(1)} %bitcast.112, s32[4096]{0:T(1024)S(1)} %reshape.114, s32[]{:T(128)} %constant.37.clone.1), kind=kCustom, calls=%fused_computation.57 | custom fusion | bytes 20484 | tf_op jit(solution)/shard_map/scatter | solution.py:182
  197.7 7.1 convert_reduce_fusion
  204.8 53.0 %all-gather.10.cloned.1.call-done.refs_0_ = bf16[16,448,1280]{2,1,0:T(8,128)(2,1)} async-done(((bf16[1,448,1280]{2,1,0:T(8,128)(2,1)}), bf16[16,448,1280]{2,1,0:T(8,128)(2,1)}) %all-gather.10.cloned.1.call-update) | async-done | bytes 18350096 | tf_op jit(solution)/shard_map/all_gather | solution.py:154
  257.8 7.7 dynamic-slice_bitcast_fusion.1
  265.6 8.4 slice.94
  275.6 8.7 fusion.2
  284.4 9.1 fusion.5
  302.6 188.9 %collective-permute-done = bf16[8,224,4096]{2,1,0:T(8,128)(2,1)} collective-permute-done((bf16[8,224,4096]{2,1,0:T(8,128)(2,1)}, bf16[8,224,4096]{2,1,0:T(8,128)(2,1)}, u32[]{:S(2)}, u32[]{:S(2)}) %collective-permute-start) | collective-permute-done | bytes 14680096 | tf_op jit(solution)/shard_map/ppermute | solution.py:157
  491.6 77.8 %gather_fusion = bf16[5120,4096]{1,0:T(8,128)(2,1)} fusion(bf16[2048,4096]{1,0:T(8,128)(2,1)} %copy-done.2, s32[5120]{0:T(1024)S(1)} %broadcast_clamp_fusion), kind=kCustom, calls=%fused_computation | custom fusion | bytes 83906560 | tf_op jit(solution)/shard_map/jit(_take)/gather | solution.py:183
  573.4 114.1 %collective-permute-done.2.refs_0_ = bf16[8,448,256]{2,1,0:T(8,128)(2,1)} collective-permute-done((bf16[8,448,256]{2,1,0:T(8,128)(2,1)S(1)}, bf16[8,448,256]{2,1,0:T(8,128)(2,1)}, u32[]{:S(2)}, u32[]{:S(2)}) %collective-permute-start.2) | collective-permute-done | bytes 1835040 | tf_op jit(solution)/shard_map/ppermute | solution.py:157
  688.0 27.0 %fusion.30 = f32[16,320,224]{2,1,0:T(8,128)} fusion(bf16[16,320,4096]{2,1,0:T(8,128)(2,1)} %bitcast.80, bf16[16,224,4096]{2,1,0:T(8,128)(2,1)} %bitcast.113), kind=kOutput, calls=%fused_computation.77 | convolution fusion | flops 9395240960 | bytes 75890688 | tf_op jit(solution)/shard_map/erd,efd->erf/dot_general | solution.py:196
  715.0 26.1 %multiply_convert_fusion = bf16[16,320,224]{2,1,0:T(8,128)(2,1)S(1)} fusion(f32[16,320,224]{2,1,0:T(8,128)} %fusion.30, bf16[16,320,4096]{2,1,0:T(8,128)(2,1)} %bitcast.81, bf16[16,224,4096]{2,1,0:T(8,128)(2,1)} %bitcast.114), kind=kOutput, calls=%fused_computation.19 | convolution fusion | flops 9402122240 | bytes 78184448 | tf_op jit(solution)/shard_map/erd,efd->erf/dot_general | solution.py:196
  741.1 26.9 %fusion.29 = f32[16,320,224]{2,1,0:T(8,128)} fusion(bf16[16,320,4096]{2,1,0:T(8,128)(2,1)} %bitcast.82, bf16[16,224,4096]{2,1,0:T(8,128)(2,1)} %bitcast.88), kind=kOutput, calls=%fused_computation.76 | convolution fusion | flops 9395240960 | bytes 75890688 | tf_op jit(solution)/shard_map/erd,efd->erf/dot_general | solution.py:196
  768.0 17.6 %fusion.8 = f32[8,320,224]{2,1,0:T(8,128)S(1)} fusion(bf16[8,224,4096]{2,1,0:T(8,128)(2,1)} %collective-permute-done, bf16[8,2,320,4096]{3,2,1,0:T(8,128)(2,1)} %bitcast.83, s32[]{:T(128)S(6)} %select_n.87), kind=kOutput, calls=%fused_computation.12 | convolution fusion | flops 4697620480 | bytes 37945348 | tf_op jit(solution)/shard_map/erd,efd->erf/dot_general | solution.py:196
  785.6 15.3 %fusion.6 = f32[8,320,224]{2,1,0:T(8,128)} fusion(bf16[8,224,4096]{2,1,0:T(8,128)(2,1)} %collective-permute-done.1, bf16[8,2,320,4096]{3,2,1,0:T(8,128)(2,1)} %bitcast.84, s32[]{:T(128)S(6)} %select_n.88), kind=kOutput, calls=%fused_computation.10 | convolution fusion | flops 4697620480 | bytes 37945348 | tf_op jit(solution)/shard_map/erd,efd->erf/dot_general | solution.py:196
  805.6 5.0 pad_maximum_fusion.act
  810.6 35.1 %shard_map.100.refs_1_ = bf16[2048,4096]{1,0:T(8,128)(2,1)} custom-call(s32[2]{0:T(128)} %pad_add_fusion.5.where, s32[2048]{0:T(1024)} %bitcast.103, s32[2048]{0:T(1024)} %bitcast.97, f32[2048]{0:T(1024)} %get-tuple-element.12.gate_a, f32[2048]{0:T(1024)} %get-tuple-element.13.gate_b, bf16[16,320,448]{2,1,0:T(8,128)(2,1)} %pad_maximum_fusion.act, ...), custom_call_target="tpu_custom_call" | custom-call | flops 4697620480 | bytes 27656192 | tf_op jit(solution)/shard_map/pallas_call | solution.py:109
  845.7 22.1 %shard_map.101.refs_2_ = bf16[2048,4096]{1,0:T(8,128)(2,1)} custom-call(s32[2]{0:T(128)} %pad_add_fusion.4.where, s32[2048]{0:T(1024)} %bitcast.104, s32[2048]{0:T(1024)} %bitcast.98, f32[2048]{0:T(1024)} %get-tuple-element.12.gate_a, f32[2048]{0:T(1024)} %get-tuple-element.13.gate_b, ...), custom_call_target="tpu_custom_call", output_to_operand_aliasing={{}: (8, {})} | custom-call | flops 1174405120 | bytes 10354688 | tf_op jit(solution)/shard_map/pallas_call | solution.py:109
  867.8 35.6 %shard_map.102.refs_1_ = bf16[2048,4096]{1,0:T(8,128)(2,1)} custom-call(s32[2]{0:T(128)} %get-tuple-element.37.where, s32[2048]{0:T(1024)} %bitcast.105, s32[2048]{0:T(1024)} %bitcast.99, f32[2048]{0:T(1024)} %get-tuple-element.12.gate_a, f32[2048]{0:T(1024)} %get-tuple-element.13.gate_b, ...), custom_call_target="tpu_custom_call", output_to_operand_aliasing={{}: (9, {})} | custom-call | flops 4697620480 | bytes 27656192 | tf_op jit(solution)/shard_map/pallas_call | solution.py:109
  903.5 35.1 %shard_map.103.refs_1_ = bf16[2048,4096]{1,0:T(8,128)(2,1)} custom-call(s32[2]{0:T(128)} %get-tuple-element.36.where, s32[2048]{0:T(1024)} %bitcast.106, s32[2048]{0:T(1024)} %bitcast.100, f32[2048]{0:T(1024)} %get-tuple-element.12.gate_a, f32[2048]{0:T(1024)} %get-tuple-element.13.gate_b, ...), custom_call_target="tpu_custom_call", output_to_operand_aliasing={{}: (8, {})} | custom-call | flops 4697620480 | bytes 27656192 | tf_op jit(solution)/shard_map/pallas_call | solution.py:109
  938.6 26.7 %shard_map.104.refs_2_ = bf16[2048,4096]{1,0:T(8,128)(2,1)} custom-call(s32[2]{0:T(128)} %get-tuple-element.35.where, s32[2048]{0:T(1024)} %bitcast.107, s32[2048]{0:T(1024)} %bitcast.101, f32[2048]{0:T(1024)} %get-tuple-element.12.gate_a, f32[2048]{0:T(1024)} %get-tuple-element.13.gate_b, ...), custom_call_target="tpu_custom_call", output_to_operand_aliasing={{}: (8, {})} | custom-call | flops 2348810240 | bytes 16121856 | tf_op jit(solution)/shard_map/pallas_call | solution.py:109
  965.4 22.1 %shard_map.105 = bf16[2048,4096]{1,0:T(8,128)(2,1)} custom-call(s32[2]{0:T(128)} %get-tuple-element.34.where, s32[2048]{0:T(1024)} %bitcast.108, s32[2048]{0:T(1024)} %bitcast.102, f32[2048]{0:T(1024)} %get-tuple-element.12.gate_a, f32[2048]{0:T(1024)} %get-tuple-element.13.gate_b, ...), custom_call_target="tpu_custom_call", output_to_operand_aliasing={{}: (9, {})} | custom-call | flops 1174405120 | bytes 10354688 | tf_op jit(solution)/shard_map/pallas_call | solution.py:109
  (95 shorter events, 43.4 us)
Async XLA Ops:
  6.5 287.0 %copy-start = (bf16[4096,16]{0,1:T(8,128)(2,1)S(1)}, bf16[4096,16]{0,1:T(8,128)(2,1)}, u32[]{:S(2)}) copy-start(bf16[4096,16]{0,1:T(8,128)(2,1)} %param.13) | copy-start | bytes 393220
  6.5 153.1 %all-gather.12.cloned.1.call-start = ((), (), s32[]{:S(2)}) async-start(), calls=%async_computation.1 | async-start | bytes 31195136 | tf_op jit(solution)/shard_map/all_gather | solution.py:154
  10.4 247.4 %all-gather.10.cloned.1.call-start = ((), (), s32[]{:S(2)}) async-start(), calls=%async_computation | async-start | bytes 19496960 | tf_op jit(solution)/shard_map/all_gather | solution.py:154
  12.9 675.1 %all-gather.14.cloned.1.call-start = ((), (), s32[]{:S(2)}) async-start(), calls=%async_computation.2 | async-start | bytes 31195136 | tf_op jit(solution)/shard_map/all_gather | solution.py:154
  15.9 699.1 %all-gather.16.cloned.1.call-start = ((), (), s32[]{:S(2)}) async-start(), calls=%async_computation.3 | async-start | bytes 31195136 | tf_op jit(solution)/shard_map/all_gather | solution.py:154
  18.9 884.6 %all-gather.18.cloned.1.call-start = ((), (), s32[]{:S(2)}) async-start(), calls=%async_computation.4 | async-start | bytes 23396352 | tf_op jit(solution)/shard_map/all_gather | solution.py:154
  159.7 14.9 %copy-start.5 = (s32[2048,2]{0,1:T(2,128)S(1)}, s32[2048,2]{0,1:T(2,128)}, u32[]{:S(2)}) copy-start(s32[2048,2]{0,1:T(2,128)} %param.17) | copy-start | bytes 49156
  173.1 318.5 %collective-permute-start = (bf16[8,224,4096]{2,1,0:T(8,128)(2,1)}, bf16[8,224,4096]{2,1,0:T(8,128)(2,1)}, u32[]{:S(2)}, u32[]{:S(2)}) collective-permute-start(bf16[8,224,4096]{2,1,0:T(8,128)(2,1)} %dynamic-slice_bitcast_fusion), channel_id=1, source_target_pairs={{0,16},{16,0},{1,17},{17,1},{2,18},{18,2},{3,19},{19,3},{4,20},{20... | collective-permute-start | bytes 44040200 | tf_op jit(solution)/shard_map/ppermute | solution.py:157
  265.6 18.8 %slice-start = ((s8[16777216]{0:T(1024)(128)(4,1)}), s8[4194304]{0:T(1024)(128)(4,1)S(1)}, s32[]{:S(2)}) async-start(s8[16777216]{0:T(1024)(128)(4,1)} %bitcast.75), calls=%async_computation.5 | async-start | bytes 8388608
  265.6 18.8 %slice-start.1 = ((s8[16777216]{0:T(1024)(128)(4,1)}), s8[4194304]{0:T(1024)(128)(4,1)S(1)}, s32[]{:S(2)}) async-start(s8[16777216]{0:T(1024)(128)(4,1)} %bitcast.75), calls=%async_computation.6 | async-start | bytes 8388608
  274.0 10.3 %slice-start.2 = ((s8[16777216]{0:T(1024)(128)(4,1)}), s8[4194304]{0:T(1024)(128)(4,1)S(1)}, s32[]{:S(2)}) async-start(s8[16777216]{0:T(1024)(128)(4,1)} %bitcast.75), calls=%async_computation.7 | async-start | bytes 8388608
  274.0 10.3 %slice-start.3 = ((s8[16777216]{0:T(1024)(128)(4,1)}), s8[4194304]{0:T(1024)(128)(4,1)S(1)}, s32[]{:S(2)}) async-start(s8[16777216]{0:T(1024)(128)(4,1)} %bitcast.75), calls=%async_computation.8 | async-start | bytes 8388608
  274.0 10.4 %copy-start.6 = (f32[4096]{0:T(1024)S(1)}, f32[4096]{0:T(1024)}, u32[]{:S(2)}) copy-start(f32[4096]{0:T(1024)} %param.12) | copy-start | bytes 49156
  274.0 10.4 %copy-start.7 = (f32[4096]{0:T(1024)S(1)}, f32[4096]{0:T(1024)}, u32[]{:S(2)}) copy-start(f32[4096]{0:T(1024)} %param.11) | copy-start | bytes 49156
  274.0 413.5 %collective-permute-start.4 = (bf16[8,448,1024]{2,1,0:T(8,128)(2,1)}, bf16[8,448,1024]{2,1,0:T(8,128)(2,1)}, u32[]{:S(2)}, u32[]{:S(2)}) collective-permute-start(bf16[8,448,1024]{2,1,0:T(8,128)(2,1)} %slice.94), channel_id=1, source_target_pairs={{0,16},{16,0},{1,17},{17,1},{2,18},{18,2},{3,19},{19,3},{4,20},{20... | collective-permute-start | bytes 22020104 | tf_op jit(solution)/shard_map/ppermute | solution.py:157
  284.4 9.2 copy-start.3
  293.6 8.9 copy-start.4
  301.4 386.1 %collective-permute-start.2 = (bf16[8,448,256]{2,1,0:T(8,128)(2,1)S(1)}, bf16[8,448,256]{2,1,0:T(8,128)(2,1)}, u32[]{:S(2)}, u32[]{:S(2)}) collective-permute-start(bf16[8,448,256]{2,1,0:T(8,128)(2,1)S(1)} %slice.92), channel_id=1, source_target_pairs={{0,16},{16,0},{1,17},{17,1},{2,18},{18,2},{3,19},{19,3},{4,20},{20... | collective-permute-start | bytes 5505032 | tf_op jit(solution)/shard_map/ppermute | solution.py:157
  491.6 294.0 %collective-permute-start.1 = (bf16[8,224,4096]{2,1,0:T(8,128)(2,1)}, bf16[8,224,4096]{2,1,0:T(8,128)(2,1)}, u32[]{:S(2)}, u32[]{:S(2)}) collective-permute-start(bf16[8,224,4096]{2,1,0:T(8,128)(2,1)} %collective-permute-done), channel_id=1, source_target_pairs={{0,1},{1,0},{2,3},{3,2},{4,5},{5,4},{6,7},{7,6},{8,9},{9,8},{10,11... | collective-permute-start | bytes 44040200 | tf_op jit(solution)/shard_map/ppermute | solution.py:158
  687.5 277.9 %collective-permute-start.3 = (bf16[8,448,256]{2,1,0:T(8,128)(2,1)}, bf16[8,448,256]{2,1,0:T(8,128)(2,1)}, u32[]{:S(2)}, u32[]{:S(2)}) collective-permute-start(bf16[8,448,256]{2,1,0:T(8,128)(2,1)} %collective-permute-done.2.refs_0_), channel_id=1, source_target_pairs={{0,1},{1,0},{2,3},{3,2},{4,5},{5,4},{6,7},{7,6},{8,9},{9,8},{10,11... | collective-permute-start | bytes 5505032 | tf_op jit(solution)/shard_map/ppermute | solution.py:158
  687.5 180.3 %collective-permute-start.5 = (bf16[8,448,1024]{2,1,0:T(8,128)(2,1)}, bf16[8,448,1024]{2,1,0:T(8,128)(2,1)}, u32[]{:S(2)}, u32[]{:S(2)}) collective-permute-start(bf16[8,448,1024]{2,1,0:T(8,128)(2,1)} %collective-permute-done.4.refs_0_), channel_id=1, source_target_pairs={{0,1},{1,0},{2,3},{3,2},{4,5},{5,4},{6,7},{7,6},{8,9},{9,8},{10,11... | collective-permute-start | bytes 22020104 | tf_op jit(solution)/shard_map/ppermute | solution.py:158
  768.0 36.3 %slice-start.4 = ((s8[5242880]{0:T(1024)(128)(4,1)}), s8[4194304]{0:T(1024)(128)(4,1)S(1)}, s32[]{:S(2)}) async-start(s8[5242880]{0:T(1024)(128)(4,1)} %bitcast.89), calls=%async_computation.9 | async-start | bytes 8388608
  785.6 18.7 %slice-start.5 = ((s8[5242880]{0:T(1024)(128)(4,1)}), s8[1048576]{0:T(1024)(128)(4,1)S(1)}, s32[]{:S(2)}) async-start(s8[5242880]{0:T(1024)(128)(4,1)} %bitcast.89), calls=%async_computation.10 | async-start | bytes 2097152
  965.4 22.2 %copy-start.1 = (bf16[4096,16]{0,1:T(8,128)(2,1)S(1)}, bf16[4096,16]{0,1:T(8,128)(2,1)}, u32[]{:S(2)}) copy-start(bf16[4096,16]{0,1:T(8,128)(2,1)} %param.13) | copy-start | bytes 393220
  (1 other events, 6.2 us)
Sparse Core Ops, SparseCore 0:
  10.6 149.0 all-gather.11
  161.3 96.5 all-gather.9
  259.4 148.1 all-gather.13
  409.1 148.2 all-gather.15
  558.8 113.7 all-gather.17

commit v3 on v2

--- a/solution.py
+++ b/solution.py
@@ -38,44 +38,42 @@
 def mix_kernel(width, weight_col, has_prev, n_weights, where, pick_a, pick_b, gate_a, gate_b, act, hidden, *refs):
     weights, refs = refs[:n_weights], refs[n_weights + (1 if has_prev else 0):]
     out, table, mix, x_buf, o_buf, w_buf, w_sem, x_sem, o_sem = refs
-    _, capacity, _ = act.shape
+    capacity = act.shape[1]
     tokens = x_buf.shape[0]
-    tiles = width // 128
     step = min(256, width)
-    block = mix.shape[0]
+    block = mix.shape[0] // 8
     col = pl.multiple_of(where[0], 128)
+
+    def load_w(source, first, i):
+        return pltpu.make_async_copy(source.at[i, :, pl.ds(weight_col, width)], w_buf.at[first + i], w_sem.at[first + i])
+
+    firsts = [sum(source.shape[0] for source in weights[:k]) for k in range(n_weights)]
+    for source, first in zip(weights, firsts):
+        for i in range(source.shape[0]):
+            load_w(source, first, i).start()
     load_x = pltpu.make_async_copy(hidden.at[:, pl.ds(col, width)], x_buf, x_sem)
     load_x.start()
 
-    def load_w(source, i, slot):
-        return pltpu.make_async_copy(source.at[i, :, pl.ds(weight_col, width)], w_buf.at[slot], w_sem.at[slot])
-
-    for k, source in enumerate(weights):
-        count = source.shape[0]
-        load_w(source, 0, 0).start()
-
-        @pl.loop(0, count)
+    for k, (source, first) in enumerate(zip(weights, firsts)):
+        @pl.loop(0, source.shape[0])
         def _(i):
-            slot = lax.rem(i, 2)
-
-            @pl.when(i + 1 < count)
-            def _():
-                load_w(source, i + 1, 1 - slot).start()
-
-            load_w(source, i, slot).wait()
+            load_w(source, first, i).wait()
             if n_weights == 1:
                 expert = i
             else:
                 expert = 2 * i + (where[1] if k == 0 else 1 - where[1])
-            rows = pl.ds(pl.multiple_of(expert * capacity, 8), capacity)
+            base = pl.multiple_of(expert * (capacity * 8), 8)
             lhs = act[expert]
             for start in range(0, width, step):
-                prod = jnp.dot(lhs, w_buf[slot, :, start:start + step], preferred_element_type=jnp.float32)
+                prod = jnp.dot(lhs, w_buf[first + i, :, start:start + step], preferred_element_type=jnp.float32)
                 prod = prod.astype(jnp.bfloat16).astype(jnp.float32)
                 for j in range(step // 128):
-                    table[rows, start // 128 + j, :] = prod[:, j * 128:(j + 1) * 128]
+                    table[pl.ds(base + start // 128 + j, capacity, stride=8), :] = prod[:, j * 128:(j + 1) * 128]
 
     load_x.wait()
+
+    def row_of(pick):
+        return table[pl.ds(pl.multiple_of(pick * 8, 8), 8), :]
 
     @pl.loop(0, tokens // block)
     def _(b):
@@ -84,14 +82,14 @@
         @pl.loop(0, block // 16)
         def _(i):
             slots = [base + i * 16 + k for k in range(16)]
-            picked = [(table[pick_a[t]], table[pick_b[t]]) for t in slots]
+            picked = [(row_of(pick_a[t]), row_of(pick_b[t])) for t in slots]
             sums = [gate_a[t] * first + gate_b[t] * second for t, (first, second) in zip(slots, picked)]
             for k in range(16):
-                mix[i * 16 + k] = sums[k]
-
-        for j in range(tiles):
+                mix[pl.ds(pl.multiple_of(i * 128 + k * 8, 8), 8), :] = sums[k]
+
+        for j in range(width // 128):
             cols = slice(j * 128, (j + 1) * 128)
-            total = x_buf[pl.ds(base, block), cols].astype(jnp.float32) + mix[:, j, :]
+            total = x_buf[pl.ds(base, block), cols].astype(jnp.float32) + mix[pl.ds(j, block, stride=8), :]
             o_buf[pl.ds(base, block), cols] = total.astype(jnp.bfloat16)
 
     store = pltpu.make_async_copy(o_buf, out.at[:, pl.ds(col, width)], o_sem)
@@ -102,7 +100,6 @@
 def mix_columns(where, picks, gates, act, hidden, weights, prev, width, weight_col=0):
     experts, capacity, ff_width = act.shape
     tokens = hidden.shape[0]
-    tiles = width // 128
     has_prev = prev is not None
     smem, vmem, hbm = [pl.BlockSpec(memory_space=space) for space in (pltpu.SMEM, pltpu.VMEM, pl.ANY)]
     operands = [where, *picks, *gates, act, hidden, *weights] + ([prev] if has_prev else [])
@@ -112,12 +109,12 @@
         in_specs=[smem] * 5 + [vmem] + [hbm] * (len(operands) - 6),
         out_specs=hbm,
         scratch_shapes=[
-            pltpu.VMEM((experts * capacity, tiles, 128), jnp.float32),
-            pltpu.VMEM((128, tiles, 128), jnp.float32),
+            pltpu.VMEM((experts * capacity * 8, 128), jnp.float32),
+            pltpu.VMEM((128 * 8, 128), jnp.float32),
             pltpu.VMEM((tokens, width), jnp.bfloat16),
             pltpu.VMEM((tokens, width), jnp.bfloat16),
-            pltpu.VMEM((2, ff_width, width), jnp.bfloat16),
-            pltpu.SemaphoreType.DMA((2,)),
+            pltpu.VMEM((experts, ff_width, width), jnp.bfloat16),
+            pltpu.SemaphoreType.DMA((experts,)),
             pltpu.SemaphoreType.DMA,
             pltpu.SemaphoreType.DMA,
         ],
@@ -144,7 +141,7 @@
         core = lax.rem(lax.axis_index("ep"), 2)
         on_left, first_core = side == 0, core == 0
 
-        ff_half, col_half = 112, 1280
+        ff_half, col_half = 104, 1280
         ff_split, col_split = 2 * ff_half, 2 * col_half
         wide = 1024
 
@@ -218,9 +215,9 @@
         out = place(None, (down_own,), own_start, wide)
         out = place(out, (down_own,), own_start + wide, slim, wide)
         out = place(out, down_wide, far_start, wide)
+        out = place(out, down_slim, far_start + wide, slim)
         out = place(out, (down_rest,), col_split, wide)
-        out = place(out, (down_rest,), col_split + wide, rest, wide)
-        return place(out, down_slim, far_start + wide, slim)
+        return place(out, (down_rest,), col_split + wide, rest, wide)
 
     return jax.shard_map(device_step, mesh=mesh,
                          in_specs=(rows_spec, P(), P(), P(), P("ep"), P("ep"), P("ep"), rows_spec, rows_spec, rows_spec),

time: 1000 us -> 913 us (0.913)
  Pallas kernels: 177 us -> 119 us
  waiting for transfers between devices: 494 us -> 461 us
    pallas_call x6, Pallas kernels: 177 us -> 119 us  [mix_columns(): pl.pallas_call(functools.partial(mix_kernel, width, weight_col, has_prev,...]
    ppermute x3, waiting for transfers between devices: 303 us -> 277 us  [swap(): far = lax.ppermute(mine, 'dp', [(0, 1), (1, 0)])]
  transfers between devices with their start and end apart: 11 -> 11, of which waited for: 4 -> 4; matrix products, arithmetic and copies ran while one was open for 30% -> 33% of each run, Pallas kernels for 16% -> 9%
where the time goes in v3:
time: 913 us; the launch traced here: 907 us
  waiting for transfers between devices  461 us (50%)
  local copies, waits for them, and re-layouts  141 us (15%)
  matrix products  119 us (13%)
  Pallas kernels  119 us (13%)
  other arithmetic  47.9 us (5%)
  between operations  13.8 us (2%)
    ppermute x3, waiting for transfers between devices, swap(): far = lax.ppermute(mine, 'dp', [(0, 1), (1, 0)])  277 us
    all_gather x5, waiting for transfers between devices, gather(): return lax.all_gather(piece[None], 'ep', axis=0, tiled=True)  184 us
    pallas_call x6, Pallas kernels, mix_columns(): pl.pallas_call(functools.partial(mix_kernel, width, weight_col, has_prev,...  119 us
    dot_general x5, matrix products, project(): jnp.einsum('erd,efd->erf', rows, weight, preferred_element_type=jnp.float32)  115 us
    gather x1, local copies, waits for them, and re-layouts, device_step(): jnp.take(normed, source_row, axis=0, mode='clip')  78.2 us
  transfers between devices with their start and end apart: 11, of which 4 were waited for; matrix products, arithmetic and copies ran while one was open for 33% of the time, Pallas kernels for 9%

profile of v3, /device:TPU:12, one launch (start us, length us, event | category | flops | bytes accessed | tf_op | source)
XLA Modules:
  0.0 906.9 jit_solution(1694127906729583264)
XLA Ops:
  21.9 127.8 %all-gather.12.cloned.1.call-done = bf16[3328,4096]{1,0:T(8,128)(2,1)} async-done(((bf16[208,4096]{1,0:T(8,128)(2,1)}), bf16[3328,4096]{1,0:T(8,128)(2,1)}) %all-gather.12.cloned.1.call-update) | async-done | bytes 27262992 | tf_op jit(solution)/shard_map/all_gather | solution.py:151
  149.7 10.4 %dynamic-slice_bitcast_fusion = bf16[8,208,4096]{2,1,0:T(8,128)(2,1)} fusion(bf16[8,2,208,4096]{3,2,1,0:T(8,128)(2,1)} %bitcast.87, s32[]{:T(128)S(6)} %select_n.87), kind=kLoop, calls=%fused_computation.16 | loop fusion | bytes 27262980 | tf_op jit(solution)/shard_map/jit(dynamic_index_in_dim)/squeeze | solution.py:158
  168.6 15.8 %scatter_custom_fusion = s32[5120]{0:T(1024)S(1)} fusion(s32[4096]{0:T(1024)S(1)} %bitcast.110, s32[4096]{0:T(1024)S(1)} %reshape.114, s32[]{:T(128)} %constant.30.clone.1), kind=kCustom, calls=%fused_computation.57 | custom fusion | bytes 20484 | tf_op jit(solution)/shard_map/scatter | solution.py:179
  184.5 7.1 convert_reduce_fusion
  191.6 56.2 %all-gather.10.cloned.1.call-done.refs_0_ = bf16[16,448,1280]{2,1,0:T(8,128)(2,1)} async-done(((bf16[1,448,1280]{2,1,0:T(8,128)(2,1)}), bf16[16,448,1280]{2,1,0:T(8,128)(2,1)}) %all-gather.10.cloned.1.call-update) | async-done | bytes 18350096 | tf_op jit(solution)/shard_map/all_gather | solution.py:151
  247.9 7.7 dynamic-slice_bitcast_fusion.1
  255.6 8.5 slice.94
  265.6 8.7 fusion.2
  274.5 9.1 %fusion.5 = bf16[2048,4096]{1,0:T(8,128)(2,1)S(1)} fusion(bf16[2048,4096]{1,0:T(8,128)(2,1)S(1)} %bitcast.76, f32[4096]{0:T(1024)S(1)} %copy-done.7, f32[4096]{0:T(1024)S(1)} %copy-done.8, f32[2048]{0:T(1024)S(1)} %add_rsqrt_fusion, f32[2048]{0:T(1024)S(1)} %broadcast_multiply_fusion), kind=kLoop, calls=%fused_computation.9 | loop fusion | flops 50331648 | bytes 33603584 | tf_op jit(solution)/shard_map/convert_element_type | solution.py:17
  294.7 161.4 %collective-permute-done = bf16[8,208,4096]{2,1,0:T(8,128)(2,1)} collective-permute-done((bf16[8,208,4096]{2,1,0:T(8,128)(2,1)}, bf16[8,208,4096]{2,1,0:T(8,128)(2,1)}, u32[]{:S(2)}, u32[]{:S(2)}) %collective-permute-start) | collective-permute-done | bytes 13631520 | tf_op jit(solution)/shard_map/ppermute | solution.py:154
  456.7 78.2 %gather_fusion = bf16[5120,4096]{1,0:T(8,128)(2,1)} fusion(bf16[2048,4096]{1,0:T(8,128)(2,1)} %copy-done.2, s32[5120]{0:T(1024)S(1)} %broadcast_clamp_fusion), kind=kCustom, calls=%fused_computation | custom fusion | bytes 83906560 | tf_op jit(solution)/shard_map/jit(_take)/gather | solution.py:180
  536.7 115.4 %collective-permute-done.2.refs_0_ = bf16[8,448,256]{2,1,0:T(8,128)(2,1)} collective-permute-done((bf16[8,448,256]{2,1,0:T(8,128)(2,1)S(1)}, bf16[8,448,256]{2,1,0:T(8,128)(2,1)}, u32[]{:S(2)}, u32[]{:S(2)}) %collective-permute-start.2) | collective-permute-done | bytes 1835040 | tf_op jit(solution)/shard_map/ppermute | solution.py:154
  652.5 27.4 %fusion.29 = f32[16,320,208]{2,1,0:T(8,128)} fusion(bf16[16,320,4096]{2,1,0:T(8,128)(2,1)} %bitcast.80, bf16[16,208,4096]{2,1,0:T(8,128)(2,1)} %bitcast.88), kind=kOutput, calls=%fused_computation.76 | convolution fusion | flops 8724152320 | bytes 73465856 | tf_op jit(solution)/shard_map/erd,efd->erf/dot_general | solution.py:193
  679.9 27.6 %fusion.30 = f32[16,320,240]{2,1,0:T(8,128)} fusion(bf16[16,320,4096]{2,1,0:T(8,128)(2,1)} %bitcast.81, bf16[16,240,4096]{2,1,0:T(8,128)(2,1)} %bitcast.111), kind=kOutput, calls=%fused_computation.77 | convolution fusion | flops 10066329600 | bytes 78315520 | tf_op jit(solution)/shard_map/erd,efd->erf/dot_general | solution.py:193
  707.5 28.2 %multiply_convert_fusion = bf16[16,320,240]{2,1,0:T(8,128)(2,1)} fusion(f32[16,320,240]{2,1,0:T(8,128)} %fusion.30, bf16[16,320,4096]{2,1,0:T(8,128)(2,1)} %bitcast.82, bf16[16,240,4096]{2,1,0:T(8,128)(2,1)} %bitcast.112), kind=kOutput, calls=%fused_computation.19 | convolution fusion | flops 10073702400 | bytes 80773120 | tf_op jit(solution)/shard_map/erd,efd->erf/dot_general | solution.py:193
  735.7 15.3 %fusion.8 = f32[8,320,208]{1,2,0:T(8,128)S(1)} fusion(bf16[8,208,4096]{2,1,0:T(8,128)(2,1)} %collective-permute-done, bf16[8,2,320,4096]{3,2,1,0:T(8,128)(2,1)} %bitcast.83, s32[]{:T(128)S(6)} %select_n.87), kind=kOutput, calls=%fused_computation.12 | convolution fusion | flops 4362076160 | bytes 36732932 | tf_op jit(solution)/shard_map/erd,efd->erf/dot_general | solution.py:193
  751.0 16.5 %fusion.6 = f32[8,320,208]{1,2,0:T(8,128)} fusion(bf16[8,208,4096]{2,1,0:T(8,128)(2,1)} %collective-permute-done.1, bf16[8,2,320,4096]{3,2,1,0:T(8,128)(2,1)} %bitcast.84, s32[]{:T(128)S(6)} %select_n.88), kind=kOutput, calls=%fused_computation.10 | convolution fusion | flops 4362076160 | bytes 36732932 | tf_op jit(solution)/shard_map/erd,efd->erf/dot_general | solution.py:193
  776.1 5.1 pad_maximum_fusion.act
  781.3 23.2 %shard_map.100.refs_1_ = bf16[2048,4096]{1,0:T(8,128)(2,1)} custom-call(s32[2]{0:T(128)} %pad_add_fusion.5.where, s32[2048]{0:T(1024)} %bitcast.101, s32[2048]{0:T(1024)} %bitcast.95, f32[2048]{0:T(1024)} %get-tuple-element.12.gate_a, f32[2048]{0:T(1024)} %get-tuple-element.13.gate_b, bf16[16,320,448]{2,1,0:T(8,128)(2,1)} %pad_maximum_fusion.act, ...), custom_call_target="tpu_custom_call" | custom-call | flops 4697620480 | bytes 27656192 | tf_op jit(solution)/shard_map/pallas_call | solution.py:106
  804.4 15.4 %shard_map.101.refs_2_ = bf16[2048,4096]{1,0:T(8,128)(2,1)} custom-call(s32[2]{0:T(128)} %pad_add_fusion.4.where, s32[2048]{0:T(1024)} %bitcast.102, s32[2048]{0:T(1024)} %bitcast.96, f32[2048]{0:T(1024)} %get-tuple-element.12.gate_a, f32[2048]{0:T(1024)} %get-tuple-element.13.gate_b, ...), custom_call_target="tpu_custom_call", output_to_operand_aliasing={{}: (8, {})} | custom-call | flops 1174405120 | bytes 10354688 | tf_op jit(solution)/shard_map/pallas_call | solution.py:106
  819.9 23.2 %shard_map.102.refs_2_ = bf16[2048,4096]{1,0:T(8,128)(2,1)} custom-call(s32[2]{0:T(128)} %pad_add_fusion.3.where, s32[2048]{0:T(1024)} %bitcast.103, s32[2048]{0:T(1024)} %bitcast.97, f32[2048]{0:T(1024)} %get-tuple-element.12.gate_a, f32[2048]{0:T(1024)} %get-tuple-element.13.gate_b, ...), custom_call_target="tpu_custom_call", output_to_operand_aliasing={{}: (9, {})} | custom-call | flops 4697620480 | bytes 27656192 | tf_op jit(solution)/shard_map/pallas_call | solution.py:106
  843.1 15.4 %shard_map.103.refs_1_ = bf16[2048,4096]{1,0:T(8,128)(2,1)} custom-call(s32[2]{0:T(128)} %pad_add_fusion.2.where, s32[2048]{0:T(1024)} %bitcast.104, s32[2048]{0:T(1024)} %bitcast.98, f32[2048]{0:T(1024)} %get-tuple-element.12.gate_a, f32[2048]{0:T(1024)} %get-tuple-element.13.gate_b, ...), custom_call_target="tpu_custom_call", output_to_operand_aliasing={{}: (9, {})} | custom-call | flops 1174405120 | bytes 10354688 | tf_op jit(solution)/shard_map/pallas_call | solution.py:106
  858.5 23.2 %shard_map.104.refs_1_ = bf16[2048,4096]{1,0:T(8,128)(2,1)} custom-call(s32[2]{0:T(128)} %get-tuple-element.35.where, s32[2048]{0:T(1024)} %bitcast.105, s32[2048]{0:T(1024)} %bitcast.99, f32[2048]{0:T(1024)} %get-tuple-element.12.gate_a, f32[2048]{0:T(1024)} %get-tuple-element.13.gate_b, ...), custom_call_target="tpu_custom_call", output_to_operand_aliasing={{}: (8, {})} | custom-call | flops 4697620480 | bytes 27656192 | tf_op jit(solution)/shard_map/pallas_call | solution.py:106
  881.7 18.3 %shard_map.105 = bf16[2048,4096]{1,0:T(8,128)(2,1)} custom-call(s32[2]{0:T(128)} %get-tuple-element.34.where, s32[2048]{0:T(1024)} %bitcast.106, s32[2048]{0:T(1024)} %bitcast.100, f32[2048]{0:T(1024)} %get-tuple-element.12.gate_a, f32[2048]{0:T(1024)} %get-tuple-element.13.gate_b, ...), custom_call_target="tpu_custom_call", output_to_operand_aliasing={{}: (8, {})} | custom-call | flops 2348810240 | bytes 16121856 | tf_op jit(solution)/shard_map/pallas_call | solution.py:106
  (94 shorter events, 48.0 us)
Async XLA Ops:
  6.5 277.1 %copy-start = (bf16[4096,16]{0,1:T(8,128)(2,1)S(1)}, bf16[4096,16]{0,1:T(8,128)(2,1)}, u32[]{:S(2)}) copy-start(bf16[4096,16]{0,1:T(8,128)(2,1)} %param.13) | copy-start | bytes 393220
  6.5 143.2 %all-gather.12.cloned.1.call-start = ((), (), s32[]{:S(2)}) async-start(), calls=%async_computation.1 | async-start | bytes 28966912 | tf_op jit(solution)/shard_map/all_gather | solution.py:151
  10.3 237.5 %all-gather.10.cloned.1.call-start = ((), (), s32[]{:S(2)}) async-start(), calls=%async_computation | async-start | bytes 19496960 | tf_op jit(solution)/shard_map/all_gather | solution.py:151
  12.8 667.1 %all-gather.14.cloned.1.call-start = ((), (), s32[]{:S(2)}) async-start(), calls=%async_computation.2 | async-start | bytes 33423360 | tf_op jit(solution)/shard_map/all_gather | solution.py:151
  15.9 691.6 %all-gather.16.cloned.1.call-start = ((), (), s32[]{:S(2)}) async-start(), calls=%async_computation.3 | async-start | bytes 33423360 | tf_op jit(solution)/shard_map/all_gather | solution.py:151
  19.0 839.5 %all-gather.18.cloned.1.call-start = ((), (), s32[]{:S(2)}) async-start(), calls=%async_computation.4 | async-start | bytes 23396352 | tf_op jit(solution)/shard_map/all_gather | solution.py:151
  149.7 11.9 %copy-start.6 = (s32[2048,2]{0,1:T(2,128)S(1)}, s32[2048,2]{0,1:T(2,128)}, u32[]{:S(2)}) copy-start(s32[2048,2]{0,1:T(2,128)} %param.17) | copy-start | bytes 49156
  160.1 296.0 %collective-permute-start = (bf16[8,208,4096]{2,1,0:T(8,128)(2,1)}, bf16[8,208,4096]{2,1,0:T(8,128)(2,1)}, u32[]{:S(2)}, u32[]{:S(2)}) collective-permute-start(bf16[8,208,4096]{2,1,0:T(8,128)(2,1)} %dynamic-slice_bitcast_fusion), channel_id=1, source_target_pairs={{0,16},{16,0},{1,17},{17,1},{2,18},{18,2},{3,19},{19,3},{4,20},{20... | collective-permute-start | bytes 40894472 | tf_op jit(solution)/shard_map/ppermute | solution.py:154
  255.6 18.8 %slice-start = ((s8[16777216]{0:T(1024)(128)(4,1)}), s8[4194304]{0:T(1024)(128)(4,1)S(1)}, s32[]{:S(2)}) async-start(s8[16777216]{0:T(1024)(128)(4,1)} %bitcast.75), calls=%async_computation.5 | async-start | bytes 8388608
  255.6 18.8 %slice-start.1 = ((s8[16777216]{0:T(1024)(128)(4,1)}), s8[4194304]{0:T(1024)(128)(4,1)S(1)}, s32[]{:S(2)}) async-start(s8[16777216]{0:T(1024)(128)(4,1)} %bitcast.75), calls=%async_computation.6 | async-start | bytes 8388608
  264.0 10.4 %slice-start.2 = ((s8[16777216]{0:T(1024)(128)(4,1)}), s8[4194304]{0:T(1024)(128)(4,1)S(1)}, s32[]{:S(2)}) async-start(s8[16777216]{0:T(1024)(128)(4,1)} %bitcast.75), calls=%async_computation.7 | async-start | bytes 8388608
  264.0 10.4 %slice-start.3 = ((s8[16777216]{0:T(1024)(128)(4,1)}), s8[4194304]{0:T(1024)(128)(4,1)S(1)}, s32[]{:S(2)}) async-start(s8[16777216]{0:T(1024)(128)(4,1)} %bitcast.75), calls=%async_computation.8 | async-start | bytes 8388608
  264.0 10.4 %copy-start.7 = (f32[4096]{0:T(1024)S(1)}, f32[4096]{0:T(1024)}, u32[]{:S(2)}) copy-start(f32[4096]{0:T(1024)} %param.12) | copy-start | bytes 49156
  264.0 10.4 %copy-start.8 = (f32[4096]{0:T(1024)S(1)}, f32[4096]{0:T(1024)}, u32[]{:S(2)}) copy-start(f32[4096]{0:T(1024)} %param.11) | copy-start | bytes 49156
  264.1 388.0 %collective-permute-start.4 = (bf16[8,448,1024]{2,1,0:T(8,128)(2,1)}, bf16[8,448,1024]{2,1,0:T(8,128)(2,1)}, u32[]{:S(2)}, u32[]{:S(2)}) collective-permute-start(bf16[8,448,1024]{2,1,0:T(8,128)(2,1)} %slice.94), channel_id=1, source_target_pairs={{0,16},{16,0},{1,17},{17,1},{2,18},{18,2},{3,19},{19,3},{4,20},{20... | collective-permute-start | bytes 22020104 | tf_op jit(solution)/shard_map/ppermute | solution.py:154
  274.4 9.2 %copy-start.4 = (s32[2048,16]{0,1:T(8,128)S(1)}, s32[2048,16]{0,1:T(8,128)}, u32[]{:S(2)}) copy-start(s32[2048,16]{0,1:T(8,128)} %param.19) | copy-start | bytes 393220
  283.6 6.2 copy-start.2
  283.6 9.6 %copy-start.5 = (s32[2048,16]{0,1:T(8,128)S(1)}, s32[2048,16]{0,1:T(8,128)}, u32[]{:S(2)}) copy-start(s32[2048,16]{0,1:T(8,128)} %param.18) | copy-start | bytes 393220
  291.5 360.6 %collective-permute-start.2 = (bf16[8,448,256]{2,1,0:T(8,128)(2,1)S(1)}, bf16[8,448,256]{2,1,0:T(8,128)(2,1)}, u32[]{:S(2)}, u32[]{:S(2)}) collective-permute-start(bf16[8,448,256]{2,1,0:T(8,128)(2,1)S(1)} %slice.93), channel_id=1, source_target_pairs={{0,16},{16,0},{1,17},{17,1},{2,18},{18,2},{3,19},{19,3},{4,20},{20... | collective-permute-start | bytes 5505032 | tf_op jit(solution)/shard_map/ppermute | solution.py:154
  456.1 294.9 %collective-permute-start.1 = (bf16[8,208,4096]{2,1,0:T(8,128)(2,1)}, bf16[8,208,4096]{2,1,0:T(8,128)(2,1)}, u32[]{:S(2)}, u32[]{:S(2)}) collective-permute-start(bf16[8,208,4096]{2,1,0:T(8,128)(2,1)} %collective-permute-done), channel_id=1, source_target_pairs={{0,1},{1,0},{2,3},{3,2},{4,5},{5,4},{6,7},{7,6},{8,9},{9,8},{10,11... | collective-permute-start | bytes 40894472 | tf_op jit(solution)/shard_map/ppermute | solution.py:155
  652.0 191.1 %collective-permute-start.3 = (bf16[8,448,256]{2,1,0:T(8,128)(2,1)}, bf16[8,448,256]{2,1,0:T(8,128)(2,1)}, u32[]{:S(2)}, u32[]{:S(2)}) collective-permute-start(bf16[8,448,256]{2,1,0:T(8,128)(2,1)} %collective-permute-done.2.refs_0_), channel_id=1, source_target_pairs={{0,1},{1,0},{2,3},{3,2},{4,5},{5,4},{6,7},{7,6},{8,9},{9,8},{10,11... | collective-permute-start | bytes 5505032 | tf_op jit(solution)/shard_map/ppermute | solution.py:155
  652.0 167.8 %collective-permute-start.5 = (bf16[8,448,1024]{2,1,0:T(8,128)(2,1)}, bf16[8,448,1024]{2,1,0:T(8,128)(2,1)}, u32[]{:S(2)}, u32[]{:S(2)}) collective-permute-start(bf16[8,448,1024]{2,1,0:T(8,128)(2,1)} %collective-permute-done.4.refs_0_), channel_id=1, source_target_pairs={{0,1},{1,0},{2,3},{3,2},{4,5},{5,4},{6,7},{7,6},{8,9},{9,8},{10,11... | collective-permute-start | bytes 22020104 | tf_op jit(solution)/shard_map/ppermute | solution.py:155
  771.4 4.7 copy-start.3
  881.7 18.4 %copy-start.1 = (bf16[4096,16]{0,1:T(8,128)(2,1)S(1)}, bf16[4096,16]{0,1:T(8,128)(2,1)}, u32[]{:S(2)}) copy-start(bf16[4096,16]{0,1:T(8,128)(2,1)} %param.13) | copy-start | bytes 393220
Sparse Core Ops, SparseCore 0:
  10.5 139.2 all-gather.11
  151.3 96.5 all-gather.9
  249.5 157.9 all-gather.13
  408.9 158.1 all-gather.15
  568.6 113.7 all-gather.17
